TPU v7x, 32 devices: a whole 2x2x4 slice. The times are simulated.
32 devices in a mesh: dp: 8 (over z, x), head: 4 (over y, core).
Axes of the slice: x: 2, y: 2, z: 4, core: 2. Of those that a mesh axis runs over, the one named last changes fastest.
Arguments:
- residual: bfloat16 [32, 4096], P('dp', 'head'), may hold values from -6 to 6
- query: bfloat16 [32, 32, 128], P('dp', 'head'), may hold values from -4.5 to 4.5
- fresh_token_keys: bfloat16 [32, 8, 128], P('dp', 'head'), may hold values from -4.5 to 4.5
- value_new: bfloat16 [32, 8, 128], P('dp', 'head'), may hold values from -24 to 24
- key_cache: bfloat16 [32, 8, 2048, 128], P('dp', 'head'), may hold values from -6 to 6
- value_cache: bfloat16 [32, 8, 2048, 128], P('dp', 'head'), may hold values from -6 to 6
- lengths: int32 [32], P('dp'), may hold values from 1024 to 2048, as said below
- pages: int32 [32, 8, 64], P('dp', 'head'), may hold values from 0 to 127, as said below
- w_out: bfloat16 [4096, 4096], P('head', 'dp'), may hold values from -0.75 to 0.75
- norm_gain: float32 [4096], P('head'), may hold values from 0.5 to 1.5
- expert_ids: int32 [32, 2], P('dp'), may hold values from 0 to 7, all different within a row; in each aligned block of 4 rows (0 to 3, 4 to 7, ...) at most 2 rows name the same one
- gate_weights: float32 [32, 2], P('dp'), may hold values from 0.1 to 1
- w_in: bfloat16 [8, 2, 4096, 7168], P('dp', None, None, 'head'), may hold values from -0.09375 to 0.09375
- w_down: bfloat16 [8, 7168, 4096], P('dp', 'head'), may hold values from -0.0625 to 0.0625
Outputs:
- layer_out: bfloat16 [32, 4096], P('dp', 'head')
Inputs may be any that keep to these rules, and one draw needn't show every extreme that they name: `lengths`: each request's length; some request has exactly 2048 and some exactly 1024. `pages`: for each request and key head, 64 distinct page numbers, all below ceil(length / 16), always including the page that holds the request's last cached token; in no fixed order. `expert_ids`: per token 2 distinct experts; among the 4 tokens of one dp index no expert is named more than 2 times.
All inputs are finite; a program needn't handle non-finite values.
Results may differ from a plain program's by a relative error of at most 0.012.
Values may be sent and summed in bfloat16 or wider, within the bound.
No kernel may reach another device: no remote copies, remote signals or barrier semaphores. Data moves between devices by JAX's collectives and lax.ppermute only.
A program may use at most 128 MiB of HBM per device.

v0:
```python
import jax
import jax.numpy as jnp
from jax import lax
from jax.sharding import PartitionSpec as P

EXPERTS = 8
TOP = 2
PAGE = 16
MOST = 2


EPSILON = 1e-05


def shards(
    residual,
    query,
    fresh_token_keys,
    value_new,
    key_cache,
    value_cache,
    lengths,
    pages,
    w_out,
    norm_gain,
    expert_ids,
    gate_weights,
    w_in,
    w_down,
):
    tok_rows = query.shape[0]
    head_local = query.shape[1]
    head_dim = query.shape[2]
    kv_local = key_cache.shape[1]
    cache_len = key_cache.shape[2]
    page_total = cache_len // PAGE
    group_member_count = head_local // kv_local
    page_numbers = jnp.arange(page_total, dtype=jnp.int32)
    page_chosen = jnp.any(pages[:, :, :, None] == page_numbers[None, None, None, :], axis=2)
    position_chosen = jnp.broadcast_to(
        page_chosen[:, :, :, None], (tok_rows, kv_local, page_total, PAGE)
    ).reshape(tok_rows, kv_local, cache_len)
    position_ids = jnp.arange(cache_len, dtype=jnp.int32)
    in_range = (position_chosen & (position_ids[None, None, :] < lengths[:, None, None]))[
        :, :, None, :
    ]
    grouped_rows = query.reshape(tok_rows, kv_local, group_member_count, head_dim)
    score_scale = head_dim ** (-0.5)
    scores = (
        jnp.einsum("bkgd,bksd->bkgs", grouped_rows, key_cache, preferred_element_type=jnp.float32)
        * score_scale
    )
    own_score = (
        jnp.einsum(
            "luxe,lue->lux", grouped_rows, fresh_token_keys, preferred_element_type=jnp.float32
        )
        * score_scale
    )
    masked = jnp.where(in_range, scores, -1e30)
    row_top = jnp.maximum(jnp.max(masked, axis=-1), own_score)
    expo = jnp.where(in_range, jnp.exp(scores - row_top[..., None]), 0.0)
    own_expo = jnp.exp(own_score - row_top)
    denominator = jnp.sum(expo, axis=-1) + own_expo
    weights = (expo / denominator[..., None]).astype(jnp.bfloat16)
    own_weight = (own_expo / denominator).astype(jnp.bfloat16)
    attended = jnp.einsum(
        "bkgs,bksd->bkgd", weights, value_cache, preferred_element_type=jnp.float32
    )
    attended = (
        attended
        + own_weight.astype(jnp.float32)[..., None] * value_new.astype(jnp.float32)[:, :, None, :]
    )
    attn_rows = attended.reshape(tok_rows, head_local * head_dim).astype(jnp.bfloat16)
    every_row = lax.all_gather(attn_rows, "dp", axis=0, tiled=True)
    column_part = jnp.dot(every_row, w_out, preferred_element_type=jnp.float32)
    head_partial = lax.all_to_all(
        column_part.astype(jnp.bfloat16), "dp", split_axis=0, concat_axis=1, tiled=True
    ).astype(column_part.dtype)
    stream = residual.astype(jnp.float32) + lax.psum_scatter(
        head_partial.astype(jnp.bfloat16), "head", scatter_dimension=1, tiled=True
    ).astype(jnp.float32)
    whole_stream, whole_gain = (
        lax.all_gather(stream, "head", axis=1, tiled=True),
        lax.all_gather(norm_gain, "head", axis=0, tiled=True),
    )
    square_mean_value = jnp.mean(whole_stream * whole_stream, axis=-1)
    normed = (
        whole_stream * lax.rsqrt(square_mean_value + EPSILON)[:, None] * whole_gain[None, :]
    ).astype(jnp.bfloat16)
    group_count = lax.axis_size("dp") // EXPERTS
    assignments = tok_rows * TOP
    flat_ids = expert_ids.reshape(assignments)
    expert_range = jnp.arange(EXPERTS, dtype=jnp.int32)
    onehot = (flat_ids[:, None] == expert_range[None, :]).astype(jnp.int32)
    earlier = jnp.cumsum(onehot, axis=0) - onehot
    slot_index = jnp.sum(earlier * onehot, axis=1)
    target = flat_ids * MOST + slot_index
    placement_map = jnp.arange(EXPERTS * MOST, dtype=jnp.int32)[:, None] == target[None, :]
    token_map = jnp.any(placement_map.reshape(EXPERTS * MOST, tok_rows, TOP), axis=2)
    outgoing = jnp.dot(
        token_map.astype(jnp.bfloat16), normed, preferred_element_type=jnp.float32
    ).astype(jnp.bfloat16)
    width_of_row = outgoing.shape[1]
    outgoing = jnp.broadcast_to(
        outgoing.reshape(EXPERTS, 1, MOST, width_of_row), (EXPERTS, group_count, MOST, width_of_row)
    )
    outgoing = outgoing.reshape(EXPERTS * group_count, MOST, width_of_row)
    arrived = lax.all_to_all(outgoing, "dp", split_axis=0, concat_axis=0, tiled=True)
    senders, slot_count, feature_count = arrived.shape
    flat_rows = arrived.reshape(senders * slot_count, feature_count)
    gate_act = jnp.dot(flat_rows, w_in[0, 0], preferred_element_type=jnp.float32)
    up_act = jnp.dot(flat_rows, w_in[0, 1], preferred_element_type=jnp.float32)
    hidden = (jax.nn.silu(gate_act) * up_act).astype(jnp.bfloat16)
    slab_out = jnp.dot(hidden, w_down[0], preferred_element_type=jnp.float32).reshape(
        senders, slot_count, w_down.shape[2]
    )
    summed_total = lax.psum_scatter(
        slab_out.astype(jnp.bfloat16), "head", scatter_dimension=2, tiled=True
    ).astype(jnp.float32)
    returned = lax.all_to_all(
        summed_total.astype(jnp.bfloat16), "dp", split_axis=0, concat_axis=0, tiled=True
    ).astype(summed_total.dtype)
    local_width = returned.shape[2]
    per_expert = jnp.sum(returned.reshape(EXPERTS, group_count, MOST, local_width), axis=1).reshape(
        EXPERTS * MOST, local_width
    )
    weighted = jnp.where(placement_map, gate_weights.reshape(assignments)[None, :], 0.0)
    combine_map = jnp.sum(weighted.reshape(EXPERTS * MOST, tok_rows, TOP), axis=2)
    mixture = jnp.dot(
        combine_map.T,
        per_expert,
        precision=lax.Precision.HIGHEST,
        preferred_element_type=jnp.float32,
    )
    return (stream + mixture).astype(jnp.bfloat16)


def solution(mesh):
    in_specs = (
        P("dp", "head"),
        P("dp", "head", None),
        P("dp", "head", None),
        P("dp", "head", None),
        P("dp", "head", None, None),
        P("dp", "head", None, None),
        P("dp"),
        P("dp", "head", None),
        P("head", "dp"),
        P("head"),
        P("dp", None),
        P("dp", None),
        P("dp", None, None, "head"),
        P("dp", "head", None),
    )
    out_specs = P("dp", "head")
    return jax.shard_map(shards, mesh=mesh, in_specs=in_specs, out_specs=out_specs, check_vma=False)
```

profile of v0, /device:TPU:0, one launch (start us, length us, event | category | flops | bytes accessed | tf_op | source)
XLA Modules:
  0.0 169.4 jit_solution(6646213300250157299)
XLA Ops:
  6.5 0.9 fusion.19
  7.5 0.2 broadcast_in_dim.28
  7.7 0.3 reshape.95
  8.0 0.7 iota_compare_fusion.1
  8.8 0.8 fusion.30
  9.6 3.5 %select_reduce_fusion = (f32[4,2,4]{2,1,0:T(2,128)S(1)}, f32[4,2,4,2048]{3,2,1,0:T(4,128)S(1)}) fusion(pred[4,2,2048]{2,1,0:T(4,128)(4,1)S(1)} %copy.32, bf16[4,2,4,128]{3,2,1,0:T(4,128)(2,1)} %bitcast.52, bf16[4,2,2048,128]{3,2,1,0:T(8,128)(2,1)} %param.18), kind=kOutput, calls=%fused_computation.19 | convolution fusion | flops 16973792 | bytes 4481152 | tf_op jit(solution)/shard_map/bkgd,bksd->bkgs/dot_general | solution.py:50
  13.1 0.3 fusion.20
  13.5 0.7 convert_element_type.55
  14.1 2.9 %fusion.18 = bf16[4,2,4,128]{3,2,1,0:T(4,128)(2,1)S(1)} fusion(bf16[4,2,2048,128]{3,2,1,0:T(8,128)(2,1)} %param.19, f32[4,2,4,2048]{3,2,1,0:T(4,128)S(1)} %get-tuple-element.8, f32[4,2,4]{2,1,0:T(2,128)S(1)} %get-tuple-element.6, f32[4,2,4]{2,1,0:T(2,128)S(1)} %multiply_maximum_fusion, pred[4,2,2048]{2,1,0:T(4,128)(4,1)S(1)} %copy.32, ...), kind=kOutput, calls=%fused_computation.17 | convolution fusion | flops 17051648 | bytes 4485504 | tf_op jit(solution)/shard_map/bkgs,bksd->bkgd/dot_general | solution.py:66
  17.1 32.4 %all-gather = bf16[8,4,1024]{2,1,0:T(4,128)(2,1)S(1)} all-gather(bf16[1,4,1024]{2,1,0:T(4,128)(2,1)S(1)} %reshape.99), channel_id=1, replica_groups=mesh['dp'=8,'head'=4] {'dp'}, dimensions={0}, use_global_device_ids=true | all-gather | bytes 73728 | tf_op jit(solution)/shard_map/all_gather | solution.py:74
  49.5 0.3 convolution_convert_fusion.1
  49.7 0.6 all_to_all.20
  50.4 5.5 %all-to-all-start = ((bf16[8,4,512]{2,1,0:T(4,128)(2,1)}), bf16[8,4,512]{2,1,0:T(4,128)(2,1)S(1)}, u32[]{:S(2)}, u32[]{:S(2)}) async-start(bf16[8,4,512]{2,1,0:T(4,128)(2,1)} %all_to_all.20), calls=%async_computation | async-start | bytes 65536 | tf_op jit(solution)/shard_map/all_to_all | solution.py:76
  55.9 0.8 copy.33
  56.8 0.2 select_reduce_fusion.2
  57.2 5.3 %all_gather.11 = f32[4096]{0:T(1024)S(1)} all-gather(f32[1024]{0:T(1024)} %param.23), channel_id=1, replica_groups=mesh['dp'=8,'head'=4] {'head'}, dimensions={0}, use_global_device_ids=true | all-gather | bytes 20480 | tf_op jit(solution)/shard_map/all_gather | solution.py:84
  62.6 1.4 copy.40
  64.1 26.2 %reduce-scatter.7.cloned.1.call-done = bf16[1024,4]{1,0:T(8,128)(2,1)} async-done(((bf16[4096,4]{1,0:T(8,128)(2,1)}), bf16[1024,4]{1,0:T(8,128)(2,1)}) %reduce-scatter.7.cloned.1.call-update) | async-done | bytes 8208
  90.3 1.1 copy.41
  91.4 0.7 convert_add_fusion
  92.1 5.2 %all_gather.10 = f32[4,4096]{1,0:T(4,128)S(1)} all-gather(f32[4,1024]{1,0:T(4,128)S(1)} %convert_add_fusion), channel_id=1, replica_groups=mesh['dp'=8,'head'=4] {'head'}, dimensions={1}, use_global_device_ids=true | all-gather | bytes 81920 | tf_op jit(solution)/shard_map/all_gather | solution.py:83
  97.3 0.1 multiply_reduce_fusion
  97.5 0.3 convolution_convert_fusion
  97.8 12.8 %all_to_all.29 = bf16[8,2,4096]{2,1,0:T(2,128)(2,1)S(1)} all-to-all(bf16[8,2,4096]{2,1,0:T(2,128)(2,1)S(1)} %reshape_reshape.3), channel_id=1, replica_groups=mesh['dp'=8,'head'=4] {'dp'}, dimensions={0} | all-to-all | bytes 262144 | tf_op jit(solution)/shard_map/all_to_all | solution.py:108
  110.7 6.2 %fusion.4 = f32[16,1792]{1,0:T(8,128)S(1)} fusion(bf16[16,4096]{1,0:T(8,128)(2,1)S(1)} %reshape.97, bf16[1,2,4096,1792]{3,2,1,0:T(8,128)(2,1)} %param.26), kind=kOutput, calls=%fused_computation.4 | convolution fusion | flops 234881024 | bytes 14925824 | tf_op jit(solution)/shard_map/dot_general | solution.py:111
  117.0 6.3 %fusion.14 = bf16[16,1792]{1,0:T(8,128)(2,1)S(1)} fusion(bf16[16,4096]{1,0:T(8,128)(2,1)S(1)} %reshape.97, bf16[1,2,4096,1792]{3,2,1,0:T(8,128)(2,1)} %param.26, f32[16,1792]{1,0:T(8,128)S(1)} %fusion.4), kind=kOutput, calls=%fused_computation.12 | convolution fusion | flops 235053056 | bytes 14983168 | tf_op jit(solution)/shard_map/dot_general | solution.py:112
  123.3 7.8 %fusion.8 = bf16[8,2,4096]{2,0,1:T(8,128)(2,1)} fusion(bf16[1,1792,4096]{2,1,0:T(8,128)(2,1)} %param.27, bf16[8,2,1792]{2,1,0:T(2,128)(2,1)S(1)} %dot_general.36), kind=kOutput, calls=%fused_computation.8 | convolution fusion | flops 234946560 | bytes 14868480 | tf_op jit(solution)/shard_map/dot_general | solution.py:114
  131.2 17.0 %reduce-scatter.5.cloned.1.call-done = bf16[8,2,1024]{2,0,1:T(8,128)(2,1)} async-done(((bf16[8,2,4096]{2,0,1:T(8,128)(2,1)}), bf16[8,2,1024]{2,0,1:T(8,128)(2,1)}) %reduce-scatter.5.cloned.1.call-update) | async-done | bytes 32784 | tf_op jit(solution)/shard_map/reduce_scatter | solution.py:117
  148.2 1.4 copy.37
  149.6 5.5 %all-to-all-start.2 = ((bf16[8,2,1024]{2,1,0:T(2,128)(2,1)}), bf16[8,2,1024]{2,1,0:T(2,128)(2,1)S(1)}, u32[]{:S(2)}, u32[]{:S(2)}) async-start(bf16[8,2,1024]{2,1,0:T(2,128)(2,1)} %copy.37), calls=%async_computation.3 | async-start | bytes 65536 | tf_op jit(solution)/shard_map/all_to_all | solution.py:120
  155.2 6.6 %all-to-all-done.2 = bf16[8,2,1024]{2,1,0:T(2,128)(2,1)S(1)} async-done(((bf16[8,2,1024]{2,1,0:T(2,128)(2,1)}), bf16[8,2,1024]{2,1,0:T(2,128)(2,1)S(1)}, u32[]{:S(2)}, u32[]{:S(2)}) %all-to-all-start.2) | async-done | bytes 32800 | tf_op jit(solution)/shard_map/all_to_all | solution.py:120
  161.8 0.7 fusion.17
  (32 shorter events, 1.0 us)
Async XLA Ops:
  6.5 42.9 %copy-start = (bf16[1024,512]{1,0:T(8,128)(2,1)S(1)}, bf16[1024,512]{1,0:T(8,128)(2,1)}, u32[]{:S(2)}) copy-start(bf16[1024,512]{1,0:T(8,128)(2,1)} %param.22) | copy-start | bytes 3145732
  50.4 12.2 %all-to-all-start = ((bf16[8,4,512]{2,1,0:T(4,128)(2,1)}), bf16[8,4,512]{2,1,0:T(4,128)(2,1)S(1)}, u32[]{:S(2)}, u32[]{:S(2)}) async-start(bf16[8,4,512]{2,1,0:T(4,128)(2,1)} %all_to_all.20), calls=%async_computation | async-start | bytes 65536 | tf_op jit(solution)/shard_map/all_to_all | solution.py:76
  55.8 34.5 %reduce-scatter.7.cloned.1.call-start = ((), (), s32[]{:S(2)}) async-start(), calls=%async_computation.6 | async-start | bytes 1310720
  64.0 84.2 %reduce-scatter.5.cloned.1.call-start = ((), (), s32[]{:S(2)}) async-start(), calls=%async_computation.5 | async-start | bytes 163840 | tf_op jit(solution)/shard_map/reduce_scatter | solution.py:117
  117.0 38.1 %copy-start.2 = (f32[4,2]{0,1:T(2,128)S(1)}, f32[4,2]{0,1:T(2,128)}, u32[]{:S(2)}) copy-start(f32[4,2]{0,1:T(2,128)} %param.25) | copy-start | bytes 100
  117.0 44.8 %copy-start.1 = (bf16[4,1024]{1,0:T(4,128)(2,1)S(1)}, bf16[4,1024]{1,0:T(4,128)(2,1)}, u32[]{:S(2)}) copy-start(bf16[4,1024]{1,0:T(4,128)(2,1)} %param.14) | copy-start | bytes 24580
  149.6 12.2 %all-to-all-start.2 = ((bf16[8,2,1024]{2,1,0:T(2,128)(2,1)}), bf16[8,2,1024]{2,1,0:T(2,128)(2,1)S(1)}, u32[]{:S(2)}, u32[]{:S(2)}) async-start(bf16[8,2,1024]{2,1,0:T(2,128)(2,1)} %copy.37), calls=%async_computation.3 | async-start | bytes 65536 | tf_op jit(solution)/shard_map/all_to_all | solution.py:120
Sparse Core Ops, SparseCore 0:
  64.1 26.1 reduce-scatter.6
  131.3 16.8 reduce-scatter.4
where the time goes:
time: 170 us; the launch traced here: 169 us
  blocking collectives  55.7 us (33%)
  waiting for transfers between devices  49.8 us (29%)
  matrix products  28.9 us (17%)
  between operations  13.6 us (8%)
  starting transfers between devices  11.1 us (7%)
  local copies, waits for them, and re-layouts  6.35 us (4%)
  other arithmetic  4 us (2%)
    all_gather x1, blocking collectives, shards(): every_row = lax.all_gather(attn_rows, 'dp', axis=0, tiled=True)  32.4 us
    unnamed x3, waiting for transfers between devices  26.2 us
    reduce_scatter x1, waiting for transfers between devices, shards(): lax.psum_scatter(slab_out.astype(jnp.bfloat16), 'head', scatter_dimension...  17 us
    all_to_all x1, blocking collectives, shards(): lax.all_to_all(outgoing, 'dp', split_axis=0, concat_axis=0, tiled=True)  12.8 us
    dot_general x1, matrix products, shards(): jnp.dot(hidden, w_down[0], preferred_element_type=jnp.float32)  7.82 us
    all_to_all x1, waiting for transfers between devices, shards(): lax.all_to_all(summed_total.astype(jnp.bfloat16), 'dp', split_axis=0, con...  6.6 us
    dot_general x1, matrix products, shards(): up_act = jnp.dot(flat_rows, w_in[0, 1], preferred_element_type=jnp.float32)  6.3 us
    dot_general x1, matrix products, shards(): jnp.dot(flat_rows, w_in[0, 0], preferred_element_type=jnp.float32)  6.24 us
  transfers between devices with their start and end apart: 4, of which 3 were waited for; matrix products, arithmetic and copies ran while one was open for 1% of the time, Pallas kernels for 0%

commit v1 on v0

v1 whole, which is shorter than its diff:
```python
import jax
import jax.numpy as jnp
from jax import lax
from jax.sharding import PartitionSpec as P

EXPERTS = 8
TOP = 2
PAGE = 16
MOST = 2
LANES = 128
BOTH = ("dp", "head")

EPSILON = 1e-05


def split3(x):
    high = lax.reduce_precision(x, 8, 7)
    mid = lax.reduce_precision(x - high, 8, 7)
    return tuple(part.astype(jnp.bfloat16) for part in (high, mid, x - high - mid))


def attend(query, fresh_token_keys, value_new, key_cache, value_cache, lengths, pages):
    tok_rows, head_local, head_dim = query.shape
    kv_local, cache_len = key_cache.shape[1:3]
    page_total = cache_len // PAGE
    group_member_count = head_local // kv_local
    page_numbers = jnp.arange(page_total, dtype=jnp.int32)
    page_chosen = jnp.any(pages[:, :, :, None] == page_numbers[None, None, None, :], axis=2)
    position_chosen = jnp.broadcast_to(
        page_chosen[:, :, :, None], (tok_rows, kv_local, page_total, PAGE)
    ).reshape(tok_rows, kv_local, cache_len)
    position_ids = jnp.arange(cache_len, dtype=jnp.int32)
    in_range = (position_chosen & (position_ids[None, None, :] < lengths[:, None, None]))[
        :, :, None, :
    ]
    grouped_rows = query.reshape(tok_rows, kv_local, group_member_count, head_dim)
    score_scale = head_dim ** (-0.5)
    scores = (
        jnp.einsum("bkgd,bksd->bkgs", grouped_rows, key_cache, preferred_element_type=jnp.float32)
        * score_scale
    )
    own_score = (
        jnp.einsum(
            "luxe,lue->lux", grouped_rows, fresh_token_keys, preferred_element_type=jnp.float32
        )
        * score_scale
    )
    masked = jnp.where(in_range, scores, -1e30)
    row_top = jnp.maximum(jnp.max(masked, axis=-1), own_score)
    expo = jnp.where(in_range, jnp.exp(scores - row_top[..., None]), 0.0)
    own_expo = jnp.exp(own_score - row_top)
    denominator = jnp.sum(expo, axis=-1) + own_expo
    weights = (expo / denominator[..., None]).astype(jnp.bfloat16)
    own_weight = (own_expo / denominator).astype(jnp.bfloat16)
    attended = jnp.einsum(
        "bkgs,bksd->bkgd", weights, value_cache, preferred_element_type=jnp.float32
    )
    attended = (
        attended
        + own_weight.astype(jnp.float32)[..., None] * value_new.astype(jnp.float32)[:, :, None, :]
    )
    return attended.reshape(tok_rows, head_local * head_dim).astype(jnp.bfloat16)


def slots_of(ids):
    owners, tok_rows, top = ids.shape
    flat = ids.reshape(owners, tok_rows * top)
    onehot = (flat[:, :, None] == jnp.arange(EXPERTS, dtype=jnp.int32)).astype(jnp.int32)
    same = (flat[:, :, None] == flat[:, None, :]).astype(jnp.int32)
    before = jnp.arange(tok_rows * top)[None, :] < jnp.arange(tok_rows * top)[:, None]
    place = jnp.sum(same * before[None].astype(jnp.int32), axis=2)
    taken = onehot[:, :, :, None] * (
        place[:, :, None, None] == jnp.arange(MOST, dtype=jnp.int32)
    ).astype(jnp.int32)
    return taken.reshape(owners, tok_rows, top, EXPERTS, MOST)


def shards(
    residual,
    query,
    fresh_token_keys,
    value_new,
    key_cache,
    value_cache,
    lengths,
    pages,
    w_out,
    norm_gain,
    expert_ids,
    gate_weights,
    w_in,
    w_down,
):
    dp_size, head_size = lax.axis_size("dp"), lax.axis_size("head")
    dp_at, head_at = lax.axis_index("dp"), lax.axis_index("head")
    group_count = dp_size // EXPERTS
    tok_rows = query.shape[0]
    batch = dp_size * tok_rows
    features = w_in.shape[2]
    col_width = w_out.shape[1]
    feat_width = residual.shape[1]
    ratio = feat_width // col_width
    half = col_width // 2
    head_rows = w_out.shape[0]

    attn_rows = attend(query, fresh_token_keys, value_new, key_cache, value_cache, lengths, pages)

    mine = (jnp.arange(head_size) == head_at)[:, None, None, None]
    residual_cut = residual.reshape(tok_rows, ratio, col_width).transpose(1, 0, 2)[None]
    residual_cut = jnp.where(mine, residual_cut, jnp.zeros((), jnp.bfloat16)).reshape(
        dp_size, tok_rows, col_width
    )
    routing = jnp.concatenate((expert_ids.astype(jnp.bfloat16),) + split3(gate_weights), axis=1)
    routing = jnp.pad(routing, ((0, 0), (0, LANES - routing.shape[1])))
    sent = jnp.concatenate(
        [
            jnp.broadcast_to(attn_rows, (dp_size,) + attn_rows.shape),
            residual_cut,
            jnp.broadcast_to(routing, (dp_size,) + routing.shape),
        ],
        axis=2,
    )
    came = lax.all_to_all(sent, "dp", split_axis=0, concat_axis=0, tiled=True)
    came = came.reshape(batch, came.shape[2])
    partial = jnp.dot(came[:, :head_rows], w_out, preferred_element_type=jnp.float32) + came[
        :, head_rows : head_rows + col_width
    ].astype(jnp.float32)
    routing = came[:, head_rows + col_width :]
    all_ids = routing[:, :TOP].astype(jnp.int32).reshape(dp_size, tok_rows, TOP)
    parts = routing[:, TOP : 4 * TOP].astype(jnp.float32).reshape(dp_size, tok_rows, 3, TOP)
    all_weights = parts[:, :, 0] + (parts[:, :, 1] + parts[:, :, 2])
    taken = slots_of(all_ids)

    gain_cut = lax.dynamic_index_in_dim(norm_gain.reshape(ratio, col_width), dp_at % ratio, 0)
    gain_cut = jnp.where(dp_at // ratio == head_at, gain_cut, 0.0)
    gain_high = lax.reduce_precision(gain_cut, 8, 7)
    partial = jnp.concatenate([partial, gain_high, gain_cut - gain_high], axis=0)
    core = head_at % 2
    kept = lax.dynamic_slice_in_dim(partial, core * half, half, axis=1)
    given = lax.dynamic_slice_in_dim(partial, (1 - core) * half, half, axis=1)
    swap = [(i, i ^ 1) for i in range(head_size)]
    chip_sum = kept + lax.ppermute(given.astype(jnp.bfloat16), "head", swap).astype(jnp.float32)
    chip_sum = chip_sum.astype(jnp.bfloat16)

    token_map = jnp.sum(taken, axis=2).astype(jnp.bfloat16)
    token_map = token_map.transpose(2, 0, 3, 1)
    own = jnp.eye(dp_size, dtype=jnp.bfloat16)
    picks = (token_map[:, :, :, None, :] * own[None, :, None, :, None]).reshape(
        EXPERTS * dp_size * MOST, batch
    )
    picked = jnp.dot(picks, chip_sum[:batch], preferred_element_type=jnp.float32)
    picked = picked.astype(jnp.bfloat16).reshape(EXPERTS, 1, 1, dp_size * MOST, half)
    gains = jnp.broadcast_to(chip_sum[batch:], (EXPERTS, 1, 1, 2, half))
    packet = jnp.concatenate([picked, gains], axis=3)
    packet = jnp.broadcast_to(
        packet, (EXPERTS, group_count, head_size) + packet.shape[3:]
    ).reshape((dp_size * head_size,) + packet.shape[3:])
    slot_rows = dp_size * MOST
    arrived = lax.all_to_all(packet, BOTH, split_axis=0, concat_axis=0, tiled=True)
    arrived = arrived.reshape(dp_size, head_size // 2, 2, slot_rows + 2, half)
    arrived = jnp.sum(arrived.astype(jnp.float32), axis=1)
    arrived = arrived.transpose(2, 0, 1, 3).reshape(slot_rows + 2, features)
    stream = arrived[:slot_rows]
    gain = arrived[slot_rows] + arrived[slot_rows + 1]
    square_mean = jnp.mean(stream * stream, axis=-1, keepdims=True)
    normed = (stream * lax.rsqrt(square_mean + EPSILON) * gain[None]).astype(jnp.bfloat16)

    gate_act = jnp.dot(normed, w_in[0, 0], preferred_element_type=jnp.float32)
    up_act = jnp.dot(normed, w_in[0, 1], preferred_element_type=jnp.float32)
    hidden = (jax.nn.silu(gate_act) * up_act).astype(jnp.bfloat16)
    slab_out = jnp.dot(hidden, w_down[0], preferred_element_type=jnp.float32)
    weighted = jnp.sum(taken.astype(jnp.float32) * all_weights[:, :, :, None, None], axis=(1, 2))
    slot_weights = lax.dynamic_index_in_dim(weighted, dp_at // group_count, 1, keepdims=False)
    slot_weights = slot_weights.reshape(slot_rows, 1)
    first = (head_at == 0) & (dp_at % group_count == 0)
    share = jnp.where(first, 1.0 / TOP, 0.0)
    given_back = (slot_weights * slab_out + share * stream).astype(jnp.bfloat16)

    given_back = given_back.reshape(dp_size, MOST, head_size, feat_width).transpose(0, 2, 1, 3)
    given_back = given_back.reshape(dp_size * head_size, MOST, feat_width)
    back = lax.all_to_all(given_back, BOTH, split_axis=0, concat_axis=0, tiled=True)
    own_map = jnp.sum(slots_of(expert_ids[None])[0], axis=1).astype(jnp.bfloat16)
    own_map = jnp.broadcast_to(
        own_map[:, :, None, None, :], (tok_rows, EXPERTS, group_count, head_size, MOST)
    ).reshape(tok_rows, dp_size * head_size * MOST)
    out = jnp.dot(
        own_map,
        back.reshape(dp_size * head_size * MOST, feat_width),
        preferred_element_type=jnp.float32,
    )
    return out.astype(jnp.bfloat16)


def solution(mesh):
    in_specs = (
        P("dp", "head"),
        P("dp", "head", None),
        P("dp", "head", None),
        P("dp", "head", None),
        P("dp", "head", None, None),
        P("dp", "head", None, None),
        P("dp"),
        P("dp", "head", None),
        P("head", "dp"),
        P("head"),
        P("dp", None),
        P("dp", None),
        P("dp", None, None, "head"),
        P("dp", "head", None),
    )
    out_specs = P("dp", "head")
    return jax.shard_map(shards, mesh=mesh, in_specs=in_specs, out_specs=out_specs, check_vma=False)
```

time: 170 us -> 80.8 us (0.48)
  blocking collectives: 55.7 us -> 0 us
  waiting for transfers between devices: 49.8 us -> 25.9 us
  between operations: 13.6 us -> 0.36 us
  other arithmetic: 4 us -> 7.59 us
  matrix products: 28.9 us -> 26.4 us
    all_gather x3 -> x0, blocking collectives: 42.9 us -> none  [the longest x1 32.4 us: shards(): every_row = lax.all_gather(attn_rows, 'dp', axis=0, tiled=True)]
    unnamed x3 -> x0, waiting for transfers between devices: 26.2 us -> none
    all_to_all x2 -> x3, waiting for transfers between devices: 6.6 us -> 25 us  [the longest x1 12.1 us: shards(): lax.all_to_all(packet, BOTH, split_axis=0, concat_axis=0, tiled=True)]
    reduce_scatter x1 -> x0, waiting for transfers between devices: 17 us -> none  [shards(): lax.psum_scatter(slab_out.astype(jnp.bfloat16), 'head', scatter_dimension...]
    all_to_all x1 -> x0, blocking collectives: 12.8 us -> none  [shards(): lax.all_to_all(outgoing, 'dp', split_axis=0, concat_axis=0, tiled=True)]
    dot_general x9 -> x8, matrix products: 28.9 us -> 26.4 us  [the longest x1 11.7 us: shards(): slab_out = jnp.dot(hidden, w_down[0], preferred_element_type=jnp.float32)]
    convert_element_type x3 -> x16, other arithmetic: 0.78 us -> 3.2 us  [the longest x2 0.83 us: slots_of(): (flat[:, :, None] == jnp.arange(EXPERTS, dtype=jnp.int32)).astype(jnp.int32)]
    unnamed x12 -> x7, local copies, waits for them, and re-layouts: 3.31 us -> 0.99 us
  transfers between devices with their start and end apart: 4 -> 4, of which waited for: 3 -> 4; matrix products, arithmetic and copies ran while one was open for 1% -> 5% of each run, Pallas kernels for 0% -> 0%
where the time goes in v1:
time: 80.8 us; the launch traced here: 80.1 us
  matrix products  26.4 us (33%)
  waiting for transfers between devices  25.9 us (32%)
  starting transfers between devices  12.5 us (15%)
  other arithmetic  7.59 us (9%)
  local copies, waits for them, and re-layouts  7.37 us (9%)
    all_to_all x1, waiting for transfers between devices, shards(): lax.all_to_all(packet, BOTH, split_axis=0, concat_axis=0, tiled=True)  12.1 us
    dot_general x1, matrix products, shards(): slab_out = jnp.dot(hidden, w_down[0], preferred_element_type=jnp.float32)  11.7 us
    all_to_all x1, waiting for transfers between devices, shards(): lax.all_to_all(given_back, BOTH, split_axis=0, concat_axis=0, tiled=True)  8 us
    all_to_all x1, starting transfers between devices, shards(): came = lax.all_to_all(sent, 'dp', split_axis=0, concat_axis=0, tiled=True)  7.28 us
    dot_general x1, matrix products, shards(): gate_act = jnp.dot(normed, w_in[0, 0], preferred_element_type=jnp.float32)  6.25 us
    all_to_all x1, waiting for transfers between devices, shards(): came = lax.all_to_all(sent, 'dp', split_axis=0, concat_axis=0, tiled=True)  4.84 us
    dot_general x1, matrix products, attend(): jnp.einsum('bkgd,bksd->bkgs', grouped_rows, key_cache, preferred_element_...  3.48 us
    dot_general x1, matrix products, attend(): jnp.einsum('bkgs,bksd->bkgd', weights, value_cache, preferred_element_typ...  2.93 us
  transfers between devices with their start and end apart: 4, of which 4 were waited for; matrix products, arithmetic and copies ran while one was open for 5% of the time, Pallas kernels for 0%

profile of v1, /device:TPU:0, one launch (start us, length us, event | category | flops | bytes accessed | tf_op | source)
XLA Modules:
  0.0 80.1 jit_solution(452940429431011822)
XLA Ops:
  0.2 0.8 convert_element_type.160
  0.9 0.7 reduce-precision_convert_fusion.1
  1.7 0.8 %fusion.26 = pred[4,2,128]{2,1,0:T(4,128)(4,1)S(1)} fusion(s32[4,2,64]{2,1,0:T(2,128)} %param.21), kind=kLoop, calls=%fused_computation.27 | loop fusion | flops 130048 | bytes 3072 | tf_op jit(solution)/shard_map/reduce_or | solution.py:28
  2.6 0.7 convert_element_type.157
  3.3 0.7 reshape.361
  4.0 0.7 iota_compare_fusion.2
  4.9 0.3 reshape.359
  5.3 0.8 %fusion.49 = f32[4,2,1,4]{3,2,1,0:T(1,128)S(1)} fusion(bf16[4,2,4,128]{3,2,1,0:T(4,128)(2,1)} %bitcast.85, bf16[4,2,128,1]{2,1,0,3:T(2,128)(2,1)} %bitcast.87), kind=kOutput, calls=%fused_computation.79 | convolution fusion | flops 8192 | bytes 10368 | tf_op jit(solution)/shard_map/luxe,lue->lux/dot_general | solution.py:43
  6.2 3.5 %select_reduce_fusion = (f32[4,2,4]{2,1,0:T(2,128)S(1)}, f32[4,2,4,2048]{3,2,1,0:T(4,128)S(1)}) fusion(pred[4,2,2048]{2,1,0:T(4,128)(4,1)S(1)} %copy.121, bf16[4,2,4,128]{3,2,1,0:T(4,128)(2,1)} %bitcast.86, bf16[4,2,2048,128]{3,2,1,0:T(8,128)(2,1)} %param.18), kind=kOutput, calls=%fused_computation.24 | convolution fusion | flops 16973792 | bytes 4481152 | tf_op jit(solution)/shard_map/bkgd,bksd->bkgs/dot_general | solution.py:39
  9.7 0.3 fusion.27
  10.0 2.9 %fusion.23 = bf16[4,2,4,128]{3,2,1,0:T(4,128)(2,1)S(1)} fusion(bf16[4,2,2048,128]{3,2,1,0:T(8,128)(2,1)} %param.19, f32[4,2,4,2048]{3,2,1,0:T(4,128)S(1)} %get-tuple-element.15, f32[4,2,4]{2,1,0:T(2,128)S(1)} %get-tuple-element.8, f32[4,2,4]{2,1,0:T(2,128)S(1)} %multiply_maximum_fusion, pred[4,2,2048]{2,1,0:T(4,128)(4,1)S(1)} %copy.121, ...), kind=kOutput, calls=%fused_computation.18 | convolution fusion | flops 17051648 | bytes 4485504 | tf_op jit(solution)/shard_map/bkgs,bksd->bkgd/dot_general | solution.py:55
  13.1 0.7 pad_maximum_fusion
  13.8 7.3 %all-to-all-start = ((bf16[8,4,1664]{2,1,0:T(4,128)(2,1)}), bf16[8,4,1664]{2,1,0:T(4,128)(2,1)S(1)}, u32[]{:S(2)}, u32[]{:S(2)}) async-start(bf16[8,4,1664]{2,1,0:T(4,128)(2,1)} %pad_maximum_fusion), calls=%async_computation | async-start | bytes 212992 | tf_op jit(solution)/shard_map/all_to_all | solution.py:123
  21.0 0.8 copy.117
  21.9 0.7 reshape.365
  22.6 0.8 fusion.46
  23.4 4.8 %all-to-all-done = bf16[8,4,1664]{2,1,0:T(4,128)(2,1)S(1)} async-done(((bf16[8,4,1664]{2,1,0:T(4,128)(2,1)}), bf16[8,4,1664]{2,1,0:T(4,128)(2,1)S(1)}, u32[]{:S(2)}, u32[]{:S(2)}) %all-to-all-start) | async-done | bytes 106528 | tf_op jit(solution)/shard_map/all_to_all | solution.py:123
  28.3 0.3 convolution_add_fusion
  28.7 0.3 select_reduce_fusion.1
  29.9 0.9 %collective-permute-done = bf16[34,256]{1,0:T(8,128)(2,1)S(1)} collective-permute-done((bf16[34,256]{1,0:T(8,128)(2,1)S(1)}, bf16[34,256]{1,0:T(8,128)(2,1)S(1)}, u32[]{:S(2)}, u32[]{:S(2)}) %collective-permute-start) | collective-permute-done | bytes 17440 | tf_op jit(solution)/shard_map/ppermute | solution.py:142
  31.0 0.8 broadcast_in_dim.122
  31.7 2.6 %all-to-all-start.1 = ((bf16[32,18,256]{2,1,0:T(8,128)(2,1)}), bf16[32,18,256]{2,1,0:T(8,128)(2,1)S(1)}, u32[]{:S(2)}, u32[]{:S(2)}) async-start(bf16[32,18,256]{2,1,0:T(8,128)(2,1)} %bitcast.13), calls=%async_computation.1 | async-start | bytes 786432 | tf_op jit(solution)/shard_map/all_to_all | solution.py:159
  35.5 12.1 %all-to-all-done.1 = bf16[32,18,256]{2,1,0:T(8,128)(2,1)S(1)} async-done(((bf16[32,18,256]{2,1,0:T(8,128)(2,1)}), bf16[32,18,256]{2,1,0:T(8,128)(2,1)S(1)}, u32[]{:S(2)}, u32[]{:S(2)}) %all-to-all-start.1) | async-done | bytes 294944 | tf_op jit(solution)/shard_map/all_to_all | solution.py:159
  47.7 0.3 reshape.373
  48.0 0.6 reduce_sum.78
  49.4 0.2 mul.183
  49.6 6.2 %fusion.4 = f32[16,1792]{1,0:T(8,128)S(1)} fusion(bf16[16,4096]{1,0:T(8,128)(2,1)S(1)} %convert_element_type.180, bf16[1,2,4096,1792]{3,2,1,0:T(8,128)(2,1)} %param.26), kind=kOutput, calls=%fused_computation.4 | convolution fusion | flops 234881024 | bytes 14925824 | tf_op jit(solution)/shard_map/dot_general | solution.py:168
  55.9 11.7 %fusion.14 = bf16[16,4096]{1,0:T(8,128)(2,1)S(1)} fusion(f32[16,4096]{1,0:T(8,128)S(1)} %mul.183, bf16[1,1792,4096]{2,1,0:T(8,128)(2,1)} %param.27, bf16[16,4096]{1,0:T(8,128)(2,1)S(1)} %convert_element_type.180, bf16[1,2,4096,1792]{3,2,1,0:T(8,128)(2,1)} %param.26, f32[16]{0:T(128)S(1)} %mul.165, f32[16,1792]{1,0:T(8,128)S(1)} %fusion.4), kind=kOutput, calls=%fused_computation.10 | convolution fusion | flops 470130688 | bytes 29999168 | tf_op jit(solution)/shard_map/dot_general | solution.py:171
  67.7 0.7 copy.136
  68.4 2.6 %all-to-all-start.2 = ((bf16[32,2,1024]{2,1,0:T(2,128)(2,1)}), bf16[32,2,1024]{2,1,0:T(2,128)(2,1)S(1)}, u32[]{:S(2)}, u32[]{:S(2)}) async-start(bf16[32,2,1024]{2,1,0:T(2,128)(2,1)} %bitcast.20), calls=%async_computation.2 | async-start | bytes 262144 | tf_op jit(solution)/shard_map/all_to_all | solution.py:181
  71.2 8.0 %all-to-all-done.2 = bf16[32,2,1024]{2,1,0:T(2,128)(2,1)S(1)} async-done(((bf16[32,2,1024]{2,1,0:T(2,128)(2,1)}), bf16[32,2,1024]{2,1,0:T(2,128)(2,1)S(1)}, u32[]{:S(2)}, u32[]{:S(2)}) %all-to-all-start.2) | async-done | bytes 131104 | tf_op jit(solution)/shard_map/all_to_all | solution.py:181
  79.3 0.8 convolution_convert_fusion.1
  (72 shorter events, 4.3 us)
Async XLA Ops:
  0.0 28.3 %copy-start = (bf16[1024,512]{1,0:T(8,128)(2,1)S(1)}, bf16[1024,512]{1,0:T(8,128)(2,1)}, u32[]{:S(2)}) copy-start(bf16[1024,512]{1,0:T(8,128)(2,1)} %param.22) | copy-start | bytes 3145732
  13.8 14.5 %all-to-all-start = ((bf16[8,4,1664]{2,1,0:T(4,128)(2,1)}), bf16[8,4,1664]{2,1,0:T(4,128)(2,1)S(1)}, u32[]{:S(2)}, u32[]{:S(2)}) async-start(bf16[8,4,1664]{2,1,0:T(4,128)(2,1)} %pad_maximum_fusion), calls=%async_computation | async-start | bytes 212992 | tf_op jit(solution)/shard_map/all_to_all | solution.py:123
  29.5 1.3 %collective-permute-start = (bf16[34,256]{1,0:T(8,128)(2,1)S(1)}, bf16[34,256]{1,0:T(8,128)(2,1)S(1)}, u32[]{:S(2)}, u32[]{:S(2)}) collective-permute-start(bf16[34,256]{1,0:T(8,128)(2,1)S(1)} %dynamic-slice_convert_fusion), channel_id=1, source_target_pairs={{0,1},{1,0},{2,3},{3,2},{4,5},{5,4},{6,7},{7,6},{8,9},{9,8},{10,11... | collective-permute-start | bytes 52232 | tf_op jit(solution)/shard_map/ppermute | solution.py:142
  31.7 15.8 %all-to-all-start.1 = ((bf16[32,18,256]{2,1,0:T(8,128)(2,1)}), bf16[32,18,256]{2,1,0:T(8,128)(2,1)S(1)}, u32[]{:S(2)}, u32[]{:S(2)}) async-start(bf16[32,18,256]{2,1,0:T(8,128)(2,1)} %bitcast.13), calls=%async_computation.1 | async-start | bytes 786432 | tf_op jit(solution)/shard_map/all_to_all | solution.py:159
  68.4 10.8 %all-to-all-start.2 = ((bf16[32,2,1024]{2,1,0:T(2,128)(2,1)}), bf16[32,2,1024]{2,1,0:T(2,128)(2,1)S(1)}, u32[]{:S(2)}, u32[]{:S(2)}) async-start(bf16[32,2,1024]{2,1,0:T(2,128)(2,1)} %bitcast.20), calls=%async_computation.2 | async-start | bytes 262144 | tf_op jit(solution)/shard_map/all_to_all | solution.py:181

commit v2 on v0

v2 whole, which is shorter than its diff:
```python
import jax
import jax.numpy as jnp
from jax import lax
from jax.experimental import pallas as pl
from jax.experimental.pallas import tpu as pltpu
from jax.sharding import Mesh
from jax.sharding import PartitionSpec as P

EXPERTS = 8
TOP = 2
PAGE = 16
MOST = 2
LANES = 128
ROWS = 8
CORES = 2

EPSILON = 1e-05
MIB = 2**20
AHEAD = 4
EARLY = 3


def in_hbm(x):
    return pltpu.with_memory_space_constraint(x, pltpu.HBM)


def in_vmem(x):
    return pltpu.with_memory_space_constraint(x, pltpu.VMEM)


class Stream:
    def __init__(self, copies, ahead):
        self.copies, self.ahead, self.at = copies, ahead, 0
        for copy in copies[:ahead]:
            copy.start()

    def next(self):
        self.copies[self.at].wait()
        if self.at + self.ahead < len(self.copies):
            self.copies[self.at + self.ahead].start()
        self.at += 1


def by_head(parts, group):
    row = lax.broadcasted_iota(jnp.int32, parts[0].shape, 0)
    whole = parts[0]
    for k in range(1, len(parts)):
        whole = jnp.where(row >= k * group, parts[k], whole)
    return whole


def over_lanes(a, b):
    return lax.dot_general(a, b, (((1,), (1,)), ((), ())), preferred_element_type=jnp.float32)


def attend_kernel(
    lengths_at, query_at, fresh_at, value_at, pages_at, residual_at, ids_at, gates_at, keys_at,
    values_at, w_out_at, gain_at, out, w_out, gain, lengths, query, fresh, value, pages, residual,
    ids, gates, keys, values, scores, small_sems, sems,
):
    tok_rows, head_local, head_dim = query.shape
    kv_local, cache_len = keys.shape[1:3]
    group = head_local // kv_local
    page_total = cache_len // PAGE
    sel = pages.shape[2]
    pairs = (
        (lengths_at, lengths), (query_at, query), (fresh_at, fresh), (value_at, value),
        (pages_at, pages), (residual_at, residual), (ids_at, ids), (gates_at, gates),
    )
    small = [pltpu.make_async_copy(a, b, small_sems.at[i]) for i, (a, b) in enumerate(pairs)]
    pairs = [(keys_at.at[b], keys.at[b]) for b in range(tok_rows)]
    pairs += [(values_at.at[b], values.at[b]) for b in range(tok_rows)]
    pairs += [(w_out_at, w_out), (gain_at, gain)]
    for copy in small:
        copy.start()
    stream = Stream(
        [pltpu.make_async_copy(a, b, sems.at[i]) for i, (a, b) in enumerate(pairs)], AHEAD
    )

    page_of = lax.broadcasted_iota(jnp.int32, (page_total, cache_len), 1) // PAGE
    page = lax.broadcasted_iota(jnp.int32, (page_total, cache_len), 0)
    spread = jnp.where(page_of == page, 1.0, 0.0).astype(jnp.bfloat16)
    page = lax.broadcasted_iota(jnp.int32, (page_total, sel), 0)
    ones = jnp.ones((head_local, sel), jnp.bfloat16)
    position = lax.broadcasted_iota(jnp.int32, (head_local, cache_len), 1)
    scale = head_dim ** (-0.5)
    for copy in small:
        copy.wait()

    def beside(ref, b):
        return jnp.concatenate([ref[b, k] for k in range(kv_local)], axis=1)

    def apart(rows):
        row = lax.broadcasted_iota(jnp.int32, rows.shape, 0)
        wide_rows = rows.astype(jnp.float32)
        return jnp.concatenate(
            [jnp.where(row // group == k, wide_rows, 0.0) for k in range(kv_local)], axis=1
        ).astype(jnp.bfloat16)

    def wide(ref, b):
        each = ref[b].astype(jnp.float32)
        return by_head(
            [jnp.broadcast_to(each[k : k + 1], (head_local, head_dim)) for k in range(kv_local)],
            group,
        )

    chosen = []
    for b in range(tok_rows):
        named = pages[b]
        hits = [
            over_lanes(
                ones, jnp.where(page == named[k : k + 1], 1.0, 0.0).astype(jnp.bfloat16)
            )
            for k in range(kv_local)
        ]
        chosen.append(by_head(hits, group).astype(jnp.bfloat16))
    chosen = jnp.dot(
        jnp.concatenate(chosen, axis=0), spread, preferred_element_type=jnp.float32
    )
    for b in range(tok_rows):
        stream.next()
        live = (chosen[b * head_local : (b + 1) * head_local] > 0.5) & (
            position < lengths[0:1, b : b + 1]
        )
        raw = over_lanes(apart(query[b]), beside(keys, b))
        scores[b] = jnp.where(live, raw * scale, -1e30)
    weights, own_weights = [], []
    for b in range(tok_rows):
        score = scores[b]
        own = jnp.sum(query[b].astype(jnp.float32) * wide(fresh, b), axis=1, keepdims=True) * scale
        top = jnp.maximum(jnp.max(score, axis=1, keepdims=True), own)
        expo = jnp.exp(score - top)
        own_expo = jnp.exp(own - top)
        total = jnp.sum(expo, axis=1, keepdims=True) + own_expo
        weights.append((expo / total).astype(jnp.bfloat16))
        own_weights.append((own_expo / total).astype(jnp.bfloat16).astype(jnp.float32))
    done = []
    for b in range(tok_rows):
        stream.next()
        both = jnp.dot(weights[b], beside(values, b), preferred_element_type=jnp.float32)
        attended = by_head(
            [both[:, k * head_dim : (k + 1) * head_dim] for k in range(kv_local)], group
        )
        attended = attended + own_weights[b] * wide(value, b)
        done.append(
            jnp.concatenate([attended[r : r + 1] for r in range(head_local)], axis=1)
        )
    done = jnp.concatenate(done, axis=0).astype(jnp.bfloat16)

    dp_size = out.shape[0]
    rows_width = head_local * head_dim
    feat_width = residual.shape[1]
    col_width = out.shape[2] - rows_width - 2 * LANES
    ratio = feat_width // col_width
    dp_at = lax.axis_index("dp")
    head_at = lax.axis_index("y") * CORES + lax.axis_index("core")
    held = residual[...]

    def lanes_of(pair):
        pad = jnp.zeros((2 * TOP, LANES - tok_rows), jnp.float32)
        packed = jnp.concatenate([jnp.concatenate(pair, axis=0), pad], axis=1)
        return pltpu.roll(packed, dp_at * tok_rows, 1).astype(jnp.bfloat16)

    gate = gates[...]
    high = gate.astype(jnp.bfloat16).astype(jnp.float32)
    mid = (gate - high).astype(jnp.bfloat16).astype(jnp.float32)
    first = lanes_of([ids[...].astype(jnp.float32), high])
    second = lanes_of([mid, gate - high - mid])
    for to in range(dp_size):
        cut = held[:, (to % ratio) * col_width : (to % ratio + 1) * col_width]
        kept = jnp.where(head_at == to // ratio, cut.astype(jnp.float32), 0.0)
        out[to, :, 0:rows_width] = done
        out[to, :, rows_width : rows_width + col_width] = kept.astype(jnp.bfloat16)
        out[to, :, rows_width + col_width : rows_width + col_width + LANES] = first
        out[to, :, rows_width + col_width + LANES :] = second
    stream.next()
    stream.next()


def attend(args, dp_size):
    query, keys, w_out, norm_gain = args[1], args[8], args[10], args[11]
    col_width = w_out.shape[1]
    tok_rows, head_local, head_dim = query.shape
    cache_len = keys.shape[2]
    width = head_local * head_dim + col_width + 2 * LANES
    return pl.pallas_call(
        attend_kernel,
        out_shape=(
            jax.ShapeDtypeStruct((dp_size, tok_rows, width), jnp.bfloat16),
            pltpu.VMEM(w_out.shape, w_out.dtype),
            pltpu.VMEM(norm_gain.shape, norm_gain.dtype),
        ),
        in_specs=[pl.BlockSpec(memory_space=pl.ANY)] * len(args),
        out_specs=(pl.BlockSpec(memory_space=pltpu.VMEM),) * 3,
        scratch_shapes=[pltpu.VMEM(a.shape, a.dtype) for a in args[:10]]
        + [
            pltpu.VMEM((tok_rows, head_local, cache_len), jnp.float32),
            pltpu.SemaphoreType.DMA((8,)),
            pltpu.SemaphoreType.DMA((2 * tok_rows + 2,)),
        ],
        compiler_params=pltpu.CompilerParams(vmem_limit_bytes=58 * MIB),
        cost_estimate=pl.CostEstimate(
            flops=4 * tok_rows * head_local * cache_len * head_dim,
            bytes_accessed=4 * keys.size + 2 * w_out.size,
            transcendentals=tok_rows * head_local * cache_len,
        ),
        name="attend",
    )(*[in_hbm(a) for a in args])


def places_of(ids, tok_rows):
    lane = lax.broadcasted_iota(jnp.int32, (1, LANES), 1)
    places = []
    for j in range(TOP):
        place = jnp.zeros((1, LANES), jnp.int32)
        for back in range(1, tok_rows):
            same = jnp.zeros((1, LANES), jnp.bool_)
            for i in range(TOP):
                same = same | (ids[j] == pltpu.roll(ids[i], back, 1))
            place = place + jnp.where(same & (lane % tok_rows >= back), 1, 0)
        places.append(place)
    return places


def project_kernel(came, w_out, norm_gain, w_in, packet, factors, early, rows, sems):
    early_copy = pltpu.make_async_copy(
        w_in.at[0, 0, :, pl.ds(0, early.shape[1])], early, sems.at[0]
    )
    early_copy.start()
    dp_size, tok_rows, width = came.shape
    depth, col_width = w_out.shape
    batch = dp_size * tok_rows
    slot_rows = dp_size * MOST
    blocks = slot_rows // ROWS
    experts_at = depth + col_width
    ratio = norm_gain.shape[1] // col_width
    dp_at = lax.axis_index("dp")
    head_at = lax.axis_index("y") * CORES + lax.axis_index("core")
    group_count = dp_size // EXPERTS
    routing = jnp.zeros((tok_rows, 2 * LANES), jnp.float32)
    for d in range(dp_size):
        each = came[d].astype(jnp.float32)
        rows[d * tok_rows : (d + 1) * tok_rows] = each[:, :experts_at]
        routing = routing + each[:, experts_at:]
    ids = [routing[j : j + 1, :LANES].astype(jnp.int32) for j in range(TOP)]
    gates = [
        routing[TOP + j : TOP + j + 1, :LANES]
        + (routing[j : j + 1, LANES:] + routing[TOP + j : TOP + j + 1, LANES:])
        for j in range(TOP)
    ]
    lane = lax.broadcasted_iota(jnp.int32, (1, LANES), 1)
    places = places_of(ids, tok_rows)

    def takes(expert, place, owner):
        hits = []
        for j in range(TOP):
            hit = (owner == lane // tok_rows) & (expert == ids[j]) & (place == places[j])
            hits.append(hit)
        return hits

    row = lax.broadcasted_iota(jnp.int32, (EXPERTS * slot_rows, LANES), 0)
    hits = takes(row // slot_rows, row % MOST, row % slot_rows // MOST)
    picks = jnp.where(hits[0] | hits[1], 1.0, 0.0)[:, :batch].astype(jnp.bfloat16)
    partial = (
        jnp.dot(
            rows[:, :depth].astype(jnp.bfloat16), w_out[...], preferred_element_type=jnp.float32
        )
        + rows[:, depth:]
    ).astype(jnp.bfloat16)
    picked = jnp.dot(picks, partial, preferred_element_type=jnp.float32).astype(jnp.bfloat16)

    gain = jnp.zeros((1, col_width), jnp.float32)
    for r in range(ratio):
        gain = jnp.where(
            dp_at % ratio == r, norm_gain[:, r * col_width : (r + 1) * col_width], gain
        )
    gain = jnp.where(dp_at // ratio == head_at, gain, 0.0)
    high = gain.astype(jnp.bfloat16).astype(jnp.float32)
    gains = [
        part[:, i * LANES : (i + 1) * LANES]
        for part in (high, gain - high)
        for i in range(col_width // LANES)
    ]
    gains = gains + [jnp.zeros((1, LANES), jnp.float32)] * (ROWS - len(gains))
    gains = jnp.concatenate(gains, axis=0).astype(jnp.bfloat16)
    copies = packet.shape[0] // EXPERTS
    for e in range(EXPERTS):
        for i in range(copies):
            to = e * copies + i
            for k in range(blocks):
                first = e * slot_rows + k * ROWS
                packet[to, :, k * col_width : (k + 1) * col_width] = picked[first : first + ROWS]
            packet[to, :, blocks * col_width :] = gains

    row = lax.broadcasted_iota(jnp.int32, (slot_rows, LANES), 0)
    hits = takes(dp_at // group_count, row % MOST, row // MOST)
    weight = sum(jnp.where(hits[j], gates[j], 0.0) for j in range(TOP))
    factors[0] = jnp.broadcast_to(jnp.sum(weight, axis=1, keepdims=True), (slot_rows, LANES))
    first = (head_at == 0) & (dp_at % group_count == 0)
    factors[1] = jnp.full((slot_rows, LANES), jnp.where(first, 1.0 / TOP, 0.0))
    early_copy.wait()


def in_cut_of(w_in):
    return 2 * LANES if w_in.shape[3] % (2 * LANES) == 0 else w_in.shape[3]


def project(came, w_out, norm_gain, w_in, y_size):
    dp_size, tok_rows = came.shape[:2]
    depth, col_width = w_out.shape
    slot_rows = dp_size * MOST
    vmem, hbm = pl.BlockSpec(memory_space=pltpu.VMEM), pl.BlockSpec(memory_space=pl.ANY)
    return pl.pallas_call(
        project_kernel,
        out_shape=(
            jax.ShapeDtypeStruct(
                (dp_size * y_size, ROWS, slot_rows // ROWS * col_width + LANES), jnp.bfloat16
            ),
            jax.ShapeDtypeStruct((2, slot_rows, LANES), jnp.float32),
            pltpu.VMEM((w_in.shape[2], in_cut_of(w_in)), w_in.dtype),
        ),
        in_specs=[vmem, vmem, vmem, hbm],
        out_specs=(vmem, vmem, vmem),
        scratch_shapes=[
            pltpu.VMEM((dp_size * tok_rows, depth + col_width), jnp.float32),
            pltpu.SemaphoreType.DMA((1,)),
        ],
        compiler_params=pltpu.CompilerParams(vmem_limit_bytes=58 * MIB),
        cost_estimate=pl.CostEstimate(
            flops=2 * dp_size * tok_rows * depth * col_width,
            bytes_accessed=2 * depth * col_width,
            transcendentals=0,
        ),
        name="project",
    )(in_vmem(came), in_vmem(w_out), in_vmem(norm_gain), in_hbm(w_in))


def cut_at(w_in, at, in_cut):
    return w_in.at[0, at % 2, :, pl.ds(at // 2 * in_cut, in_cut)]


def early_kernel(arrived, w_in, early, sems):
    copies = [
        pltpu.make_async_copy(cut_at(w_in, 1 + i, early.shape[2]), early.at[i], sems.at[i])
        for i in range(early.shape[0])
    ]
    for copy in copies:
        copy.start()
    for copy in copies:
        copy.wait()


def load_early(arrived, w_in):
    count = min(EARLY, 2 * (w_in.shape[3] // in_cut_of(w_in))) - 1
    shape = (count, w_in.shape[2], in_cut_of(w_in))
    hbm = pl.BlockSpec(memory_space=pl.ANY)
    return pl.pallas_call(
        early_kernel,
        out_shape=pltpu.VMEM(shape, w_in.dtype),
        in_specs=[hbm, hbm],
        out_specs=pl.BlockSpec(memory_space=pltpu.VMEM),
        scratch_shapes=[pltpu.SemaphoreType.DMA((count,))],
        compiler_params=pltpu.CompilerParams(vmem_limit_bytes=1 * MIB),
        cost_estimate=pl.CostEstimate(
            flops=32 * shape[0] * shape[1] * shape[2],
            bytes_accessed=2 * shape[0] * shape[1] * shape[2],
            transcendentals=0,
        ),
        name="load_early",
    )(arrived, in_hbm(w_in))


def expert_kernel(
    arrived, swapped, factors, first_in, early_in, w_in, w_down, out, ins, downs, total, x,
    normed, hidden, in_sems, down_sems,
):
    slot_rows, features = x.shape
    in_cut = ins.shape[2]
    held = 1 + early_in.shape[0]
    in_count = hidden.shape[1] // in_cut
    down_count, down_cut = downs.shape[:2]
    copies = [
        pltpu.make_async_copy(cut_at(w_in, held + i, in_cut), ins.at[i], in_sems.at[i])
        for i in range(2 * in_count - held)
    ]
    copies += [
        pltpu.make_async_copy(
            w_down.at[0, pl.ds(j * down_cut, down_cut)], downs.at[j], down_sems.at[j]
        )
        for j in range(down_count)
    ]
    stream = Stream(copies, AHEAD)
    most, feat_width = out.shape[1:]
    heads = features // feat_width
    y_size = heads // CORES
    dp_size = arrived.shape[0] // y_size
    col_width = features // dp_size
    blocks = slot_rows // ROWS
    square = jnp.zeros((slot_rows, 1), jnp.float32)
    gain = []
    for d in range(dp_size):
        piece = jnp.zeros(arrived.shape[1:], jnp.float32)
        for y in range(y_size):
            at = d * y_size + y
            piece = piece + arrived[at].astype(jnp.float32)
            piece = piece + swapped[at].astype(jnp.float32)
        slots = jnp.concatenate(
            [piece[:, k * col_width : (k + 1) * col_width] for k in range(blocks)], axis=0
        )
        square = square + jnp.sum(slots * slots, axis=1, keepdims=True)
        x[:, d * col_width : (d + 1) * col_width] = slots
        terms = piece[:, blocks * col_width :]
        count = col_width // LANES
        for i in range(count):
            gain.append(terms[i : i + 1] + terms[count + i : count + i + 1])
    scale = lax.rsqrt(square * (1.0 / features) + EPSILON)
    for i in range(features // LANES):
        cut = slice(i * LANES, (i + 1) * LANES)
        normed[:, cut] = (x[:, cut] * scale * gain[i]).astype(jnp.bfloat16)
    for j in range(in_count):
        acts = []
        for i in range(2):
            at = 2 * j + i
            if at == 0:
                cut = first_in[...]
            elif at < held:
                cut = early_in[at - 1]
            else:
                stream.next()
                cut = ins[at - held]
            acts.append(jnp.dot(normed[...], cut, preferred_element_type=jnp.float32))
        hidden[:, j * in_cut : (j + 1) * in_cut] = (jax.nn.silu(acts[0]) * acts[1]).astype(
            jnp.bfloat16
        )
    weight, part = factors[0, :, 0:1], factors[1, :, 0:1]
    for j in range(down_count):
        stream.next()
        share = jnp.dot(
            hidden[:, j * down_cut : (j + 1) * down_cut],
            downs[j],
            preferred_element_type=jnp.float32,
        )
        total[...] = share if j == 0 else total[...] + share
    for h in range(heads):
        cut = slice(h * feat_width, (h + 1) * feat_width)
        given = weight * total[:, cut] + part * x[:, cut]
        for o in range(slot_rows // most):
            out[o * heads + h] = given[o * most : (o + 1) * most].astype(jnp.bfloat16)


def experts(arrived, swapped, factors, first_in, early_in, w_in, w_down, dp_size, feat_width):
    features, width = w_in.shape[2:]
    slot_rows = factors.shape[1]
    in_cut = in_cut_of(w_in)
    left = 2 * (width // in_cut) - 1 - early_in.shape[0]
    vmem, hbm = pl.BlockSpec(memory_space=pltpu.VMEM), pl.BlockSpec(memory_space=pl.ANY)
    return pl.pallas_call(
        expert_kernel,
        out_shape=jax.ShapeDtypeStruct(
            (dp_size * (features // feat_width), MOST, feat_width), jnp.bfloat16
        ),
        in_specs=[vmem] * 5 + [hbm] * 2,
        out_specs=vmem,
        scratch_shapes=[
            pltpu.VMEM((max(left, 1), features, in_cut), jnp.bfloat16),
            pltpu.VMEM((width // in_cut, in_cut, features), jnp.bfloat16),
            pltpu.VMEM((slot_rows, features), jnp.float32),
            pltpu.VMEM((slot_rows, features), jnp.float32),
            pltpu.VMEM((slot_rows, features), jnp.bfloat16),
            pltpu.VMEM((slot_rows, width), jnp.bfloat16),
            pltpu.SemaphoreType.DMA((max(left, 1),)),
            pltpu.SemaphoreType.DMA((width // in_cut,)),
        ],
        compiler_params=pltpu.CompilerParams(vmem_limit_bytes=48 * MIB),
        cost_estimate=pl.CostEstimate(
            flops=6 * slot_rows * features * width,
            bytes_accessed=6 * features * width,
            transcendentals=slot_rows * width,
        ),
        name="experts",
    )(
        in_vmem(arrived),
        in_vmem(swapped),
        in_vmem(factors),
        in_vmem(first_in),
        in_vmem(early_in),
        in_hbm(w_in),
        in_hbm(w_down),
    )


def combine_kernel(back, ids_at, out, rows):
    sources, most, feat_width = back.shape
    tok_rows = out.shape[0]
    pad = jnp.full((TOP, LANES - tok_rows), -1, jnp.int32)
    named = jnp.concatenate([ids_at[...], pad], axis=1)
    ids = [named[j : j + 1] for j in range(TOP)]
    places = places_of(ids, tok_rows)
    row = lax.broadcasted_iota(jnp.int32, (sources * most, LANES), 0)
    expert, place = row // (sources * most // EXPERTS), row % most
    takes = jnp.zeros(row.shape, jnp.float32)
    for j in range(TOP):
        takes = jnp.where((expert == ids[j]) & (place == places[j]), 1.0, takes)
    takes = jnp.transpose(takes)[:ROWS].astype(jnp.bfloat16)
    for i in range(sources):
        rows[i * most : (i + 1) * most] = back[i].astype(jnp.float32)
    total = jnp.dot(takes, rows[...].astype(jnp.bfloat16), preferred_element_type=jnp.float32)
    out[...] = total[:tok_rows].astype(jnp.bfloat16)


def combine(back, ids):
    sources, most, feat_width = back.shape
    tok_rows = ids.shape[1]
    vmem = pl.BlockSpec(memory_space=pltpu.VMEM)
    return pl.pallas_call(
        combine_kernel,
        out_shape=jax.ShapeDtypeStruct((tok_rows, feat_width), jnp.bfloat16),
        in_specs=[vmem, vmem],
        out_specs=vmem,
        scratch_shapes=[pltpu.VMEM((sources * most, feat_width), jnp.float32)],
        compiler_params=pltpu.CompilerParams(vmem_limit_bytes=16 * MIB),
        cost_estimate=pl.CostEstimate(
            flops=2 * tok_rows * back.size, bytes_accessed=2 * back.size, transcendentals=0
        ),
        name="combine",
    )(back, ids)


def shards(
    residual,
    query,
    fresh_token_keys,
    value_new,
    key_cache,
    value_cache,
    lengths,
    pages,
    w_out,
    norm_gain,
    expert_ids,
    gate_weights,
    w_in,
    w_down,
):
    dp_size, y_size = lax.axis_size("dp"), lax.axis_size("y")
    tok_rows, feat_width = residual.shape

    sent, w_out, norm_gain = attend(
        (
            lengths.reshape(1, tok_rows),
            query,
            fresh_token_keys,
            value_new,
            pages,
            residual,
            expert_ids.T,
            gate_weights.T,
            key_cache,
            value_cache,
            w_out,
            norm_gain.reshape(1, feat_width),
        ),
        dp_size,
    )
    came = lax.all_to_all(sent, "dp", split_axis=0, concat_axis=0, tiled=True)

    packet, factors, first_in = project(came, w_out, norm_gain, w_in, y_size)
    arrived = lax.all_to_all(packet, ("dp", "y"), split_axis=0, concat_axis=0, tiled=True)
    swapped = lax.ppermute(arrived, "core", [(i, i ^ 1) for i in range(CORES)])
    early_in = load_early(arrived, w_in)
    given_back = experts(
        arrived, swapped, factors, first_in, early_in, w_in, w_down, dp_size, feat_width
    )

    back = lax.all_to_all(
        given_back, ("dp", "y", "core"), split_axis=0, concat_axis=0, tiled=True
    )
    return combine(back, expert_ids.T)


def solution(mesh):
    dp_size, head_size = mesh.shape["dp"], mesh.shape["head"]
    grid = Mesh(mesh.devices.reshape(dp_size, head_size // CORES, CORES), ("dp", "y", "core"))
    head = ("y", "core")
    in_specs = (
        P("dp", head),
        P("dp", head, None),
        P("dp", head, None),
        P("dp", head, None),
        P("dp", head, None, None),
        P("dp", head, None, None),
        P("dp"),
        P("dp", head, None),
        P(head, "dp"),
        P(head),
        P("dp", None),
        P("dp", None),
        P("dp", None, None, head),
        P("dp", head, None),
    )
    return jax.shard_map(
        shards, mesh=grid, in_specs=in_specs, out_specs=P("dp", head), check_vma=False
    )
```

time: 170 us -> 64.6 us (0.38)
  waiting for transfers between devices: 49.8 us -> 0.01 us
  matrix products: 28.9 us -> 0 us
  Pallas kernels: 0 us -> 25.8 us
  blocking collectives: 55.7 us -> 38.4 us
  between operations: 13.6 us -> 0.06 us
  starting transfers between devices: 11.1 us -> 0.01 us
  local copies, waits for them, and re-layouts: 6.35 us -> 0.01 us
  other arithmetic: 4 us -> 0 us
    all_gather x3 -> x0, blocking collectives: 42.9 us -> none  [the longest x1 32.4 us: shards(): every_row = lax.all_gather(attn_rows, 'dp', axis=0, tiled=True)]
    dot_general x9 -> x0, matrix products: 28.9 us -> none  [the longest x1 7.82 us: shards(): jnp.dot(hidden, w_down[0], preferred_element_type=jnp.float32)]
    unnamed x3 -> x0, waiting for transfers between devices: 26.2 us -> none
    pallas_call x0 -> x5, Pallas kernels: none -> 25.8 us  [the longest x1 13.9 us: experts(): pl.pallas_call(expert_kernel, out_shape=jax.ShapeDtypeStruct((dp_size * (...]
    all_to_all x1 -> x3, blocking collectives: 12.8 us -> 38.4 us  [the longest x1 14.5 us: shards(): came = lax.all_to_all(sent, 'dp', split_axis=0, concat_axis=0, tiled=True)]
    reduce_scatter x1 -> x0, waiting for transfers between devices: 17 us -> none  [shards(): lax.psum_scatter(slab_out.astype(jnp.bfloat16), 'head', scatter_dimension...]
    all_to_all x2 -> x0, starting transfers between devices: 11 us -> none  [the longest x1 5.51 us: shards(): lax.all_to_all(summed_total.astype(jnp.bfloat16), 'dp', split_axis=0, con...]
    all_to_all x2 -> x0, waiting for transfers between devices: 6.6 us -> none  [the longest x1 6.6 us: shards(): lax.all_to_all(summed_total.astype(jnp.bfloat16), 'dp', split_axis=0, con...]
  transfers between devices with their start and end apart: 4 -> 1, of which waited for: 3 -> 0; matrix products, arithmetic and copies ran while one was open for 1% -> 0% of each run, Pallas kernels for 0% -> 4%
where the time goes in v2:
time: 64.6 us; the launch traced here: 64.2 us
  blocking collectives  38.4 us (59%)
  Pallas kernels  25.8 us (40%)
    all_to_all x1, blocking collectives, shards(): came = lax.all_to_all(sent, 'dp', split_axis=0, concat_axis=0, tiled=True)  14.5 us
    pallas_call x1, Pallas kernels, experts(): pl.pallas_call(expert_kernel, out_shape=jax.ShapeDtypeStruct((dp_size * (...  13.9 us
    all_to_all x1, blocking collectives, shards(): lax.all_to_all(packet, ('dp', 'y'), split_axis=0, concat_axis=0, tiled=True)  12.9 us
    all_to_all x1, blocking collectives, shards(): lax.all_to_all(given_back, ('dp', 'y', 'core'), split_axis=0, concat_axis...  10.9 us
    pallas_call x1, Pallas kernels, attend(): pl.pallas_call(attend_kernel, out_shape=(jax.ShapeDtypeStruct((dp_size, t...  6.26 us
    pallas_call x1, Pallas kernels, project(): pl.pallas_call(project_kernel, out_shape=(jax.ShapeDtypeStruct((dp_size *...  2.48 us
    pallas_call x1, Pallas kernels, load_early(): pl.pallas_call(early_kernel, out_shape=pltpu.VMEM(shape, w_in.dtype), in_...  2.27 us
  transfers between devices with their start and end apart: 1, of which 0 were waited for; matrix products, arithmetic and copies ran while one was open for 0% of the time, Pallas kernels for 4%

profile of v2, /device:TPU:0, one launch (start us, length us, event | category | flops | bytes accessed | tf_op | source)
XLA Modules:
  0.0 64.2 jit_solution(414962911354043637)
XLA Ops:
  0.0 6.3 %attend.1 = (bf16[8,4,1792]{2,1,0:T(4,128)(2,1)}, bf16[1024,512]{1,0:T(8,128)(2,1)S(1)}, f32[1,1024]{1,0:T(1,128)S(1)}) custom-call(s32[1,4]{1,0:T(1,128)} %bitcast.8, bf16[4,8,128]{2,1,0:T(8,128)(2,1)} %query_at.1, bf16[4,2,128]{2,1,0:T(2,128)(2,1)} %fresh_at.1, bf16[4,2,128]{2,1,0:T(2,128)(2,1)} %value_at.1, s32[4,2,64]{2,1,0:T(2,128)} %pages_at.1, ...), custom_call_target="tpu_custom_call" | custom-call | flops 33554432 | bytes 9437184 | tf_op jit(solution)/shard_map/attend/pallas_call | solution.py:186
  6.3 14.5 %all_to_all.15.came = bf16[8,4,1792]{2,1,0:T(4,128)(2,1)S(1)} all-to-all(bf16[8,4,1792]{2,1,0:T(4,128)(2,1)} %get-tuple-element.11), channel_id=1, replica_groups=mesh['dp'=8,'y'=2,'core'=2] {'dp'}, dimensions={0} | all-to-all | bytes 229376 | tf_op jit(solution)/shard_map/all_to_all | solution.py:565
  20.8 2.5 %project.1 = (bf16[16,8,1152]{2,1,0:T(8,128)(2,1)}, f32[2,16,128]{2,1,0:T(8,128)}, bf16[4096,256]{1,0:T(8,128)(2,1)S(1)}) custom-call(bf16[8,4,1792]{2,1,0:T(4,128)(2,1)S(1)} %all_to_all.15.came, bf16[1024,512]{1,0:T(8,128)(2,1)S(1)} %get-tuple-element.12.w_out, f32[1,1024]{1,0:T(1,128)S(1)} %get-tuple-element.13.norm_gain, bf16[1,2,4096,1792]{3,2,1,0:T(8,128)(2,1)} %w_in.5), custom_call_target="tpu_custom_call" | custom-call | flops 33554432 | bytes 1048576 | tf_op jit(solution)/shard_map/project/pallas_call | solution.py:313
  23.3 12.9 %all_to_all.16.arrived = bf16[16,8,1152]{2,1,0:T(8,128)(2,1)S(1)} all-to-all(bf16[16,8,1152]{2,1,0:T(8,128)(2,1)} %get-tuple-element.14), channel_id=1, replica_groups=mesh['dp'=8,'y'=2,'core'=2] {'dp','y'}, dimensions={0} | all-to-all | bytes 589824 | tf_op jit(solution)/shard_map/all_to_all | solution.py:568
  36.2 0.0 copy-start
  36.2 0.0 collective-permute-start
  36.2 2.3 %load_early.1.early_in = bf16[2,4096,256]{2,1,0:T(8,128)(2,1)S(1)} custom-call(bf16[16,8,1152]{2,1,0:T(8,128)(2,1)S(1)} %all_to_all.16.arrived, bf16[1,2,4096,1792]{3,2,1,0:T(8,128)(2,1)} %w_in.5), custom_call_target="tpu_custom_call" | custom-call | flops 67108864 | bytes 4194304 | tf_op jit(solution)/shard_map/load_early/pallas_call | solution.py:357
  38.5 0.0 collective-permute-done.swapped
  38.5 0.0 copy-done
  38.5 0.0 copy-start.1
  38.5 13.9 %experts.1 = bf16[32,2,1024]{2,1,0:T(2,128)(2,1)} custom-call(bf16[16,8,1152]{2,1,0:T(8,128)(2,1)S(1)} %all_to_all.16.arrived, bf16[16,8,1152]{2,1,0:T(8,128)(2,1)S(1)} %collective-permute-done.swapped, f32[2,16,128]{2,1,0:T(8,128)S(1)} %copy-done, bf16[4096,256]{1,0:T(8,128)(2,1)S(1)} %get-tuple-element.16.first_in, ...), custom_call_target="tpu_custom_call" | custom-call | flops 704643072 | bytes 44040192 | tf_op jit(solution)/shard_map/experts/pallas_call | solution.py:457
  52.4 10.9 %all_to_all.17.back = bf16[32,2,1024]{2,1,0:T(2,128)(2,1)S(1)} all-to-all(bf16[32,2,1024]{2,1,0:T(2,128)(2,1)} %experts.1), channel_id=1, replica_groups=mesh['dp'=8,'y'=2,'core'=2] {'dp','y','core'}, dimensions={0} | all-to-all | bytes 262144 | tf_op jit(solution)/shard_map/all_to_all | solution.py:575
  63.3 0.0 copy-done.1
  63.3 0.9 %combine.1 = bf16[4,1024]{1,0:T(4,128)(2,1)} custom-call(bf16[32,2,1024]{2,1,0:T(2,128)(2,1)S(1)} %all_to_all.17.back, s32[2,4]{1,0:T(2,128)S(1)} %bitcast.5), custom_call_target="tpu_custom_call" | custom-call | flops 524288 | bytes 131072 | tf_op jit(solution)/shard_map/combine/pallas_call | solution.py:515
Async XLA Ops:
  36.2 2.3 %copy-start = (f32[2,16,128]{2,1,0:T(8,128)S(1)}, f32[2,16,128]{2,1,0:T(8,128)}, u32[]{:S(2)}) copy-start(f32[2,16,128]{2,1,0:T(8,128)} %get-tuple-element.15.factors) | copy-start | bytes 49156
  36.2 2.3 %collective-permute-start = (bf16[16,8,1152]{2,1,0:T(8,128)(2,1)S(1)}, bf16[16,8,1152]{2,1,0:T(8,128)(2,1)S(1)}, u32[]{:S(2)}, u32[]{:S(2)}) collective-permute-start(bf16[16,8,1152]{2,1,0:T(8,128)(2,1)S(1)} %all_to_all.16.arrived), channel_id=1, source_target_pairs={{0,1},{1,0},{2,3},{3,2},{4,5},{5,4},{6,7},{7,6},{8,9},{9,8},{10,11... | collective-permute-start | bytes 884744 | tf_op jit(solution)/shard_map/ppermute | solution.py:569
  38.5 24.8 %copy-start.1 = (s32[4,2]{0,1:T(2,128)S(1)}, s32[4,2]{0,1:T(2,128)}, u32[]{:S(2)}) copy-start(s32[4,2]{0,1:T(2,128)} %param.24) | copy-start | bytes 100

commit v3 on v2

--- a/solution.py
+++ b/solution.py
@@ -28,6 +28,14 @@
     return pltpu.with_memory_space_constraint(x, pltpu.VMEM)
 
 
+def in_cut_of(w_in):
+    return 2 * LANES if w_in.shape[3] % (2 * LANES) == 0 else w_in.shape[3]
+
+
+def cut_at(w_in, at, in_cut):
+    return w_in.at[0, at % 2, :, pl.ds(at // 2 * in_cut, in_cut)]
+
+
 class Stream:
     def __init__(self, copies, ahead):
         self.copies, self.ahead, self.at = copies, ahead, 0
@@ -55,7 +63,7 @@
 
 def attend_kernel(
     lengths_at, query_at, fresh_at, value_at, pages_at, residual_at, ids_at, gates_at, keys_at,
-    values_at, w_out_at, gain_at, out, w_out, gain, lengths, query, fresh, value, pages, residual,
+    values_at, w_out_at, gain_at, w_in, sent, w_out, gain, first_in, out, lengths, query, fresh, value, pages, residual,
     ids, gates, keys, values, scores, small_sems, sems,
 ):
     tok_rows, head_local, head_dim = query.shape
@@ -68,13 +76,16 @@
         (pages_at, pages), (residual_at, residual), (ids_at, ids), (gates_at, gates),
     )
     small = [pltpu.make_async_copy(a, b, small_sems.at[i]) for i, (a, b) in enumerate(pairs)]
-    pairs = [(keys_at.at[b], keys.at[b]) for b in range(tok_rows)]
-    pairs += [(values_at.at[b], values.at[b]) for b in range(tok_rows)]
-    pairs += [(w_out_at, w_out), (gain_at, gain)]
+    span = tok_rows // (sems.shape[0] // 2 - 1)
+    cuts = [pl.ds(b, span) for b in range(0, tok_rows, span)]
+    pairs = [(keys_at.at[cut], keys.at[cut]) for cut in cuts]
+    pairs += [(values_at.at[cut], values.at[cut]) for cut in cuts]
+    pairs += [(w_out_at, w_out), (cut_at(w_in, 0, first_in.shape[1]), first_in)]
+    small.append(pltpu.make_async_copy(gain_at, gain, small_sems.at[len(small)]))
     for copy in small:
         copy.start()
     stream = Stream(
-        [pltpu.make_async_copy(a, b, sems.at[i]) for i, (a, b) in enumerate(pairs)], AHEAD
+        [pltpu.make_async_copy(a, b, sems.at[i]) for i, (a, b) in enumerate(pairs)], 3
     )
 
     page_of = lax.broadcasted_iota(jnp.int32, (page_total, cache_len), 1) // PAGE
@@ -118,7 +129,8 @@
         jnp.concatenate(chosen, axis=0), spread, preferred_element_type=jnp.float32
     )
     for b in range(tok_rows):
-        stream.next()
+        if b % span == 0:
+            stream.next()
         live = (chosen[b * head_local : (b + 1) * head_local] > 0.5) & (
             position < lengths[0:1, b : b + 1]
         )
@@ -136,7 +148,8 @@
         own_weights.append((own_expo / total).astype(jnp.bfloat16).astype(jnp.float32))
     done = []
     for b in range(tok_rows):
-        stream.next()
+        if b % span == 0:
+            stream.next()
         both = jnp.dot(weights[b], beside(values, b), preferred_element_type=jnp.float32)
         attended = by_head(
             [both[:, k * head_dim : (k + 1) * head_dim] for k in range(kv_local)], group
@@ -174,29 +187,36 @@
         out[to, :, rows_width + col_width : rows_width + col_width + LANES] = first
         out[to, :, rows_width + col_width + LANES :] = second
     stream.next()
+    packet_copy = pltpu.make_async_copy(out, sent, small_sems.at[len(small)])
+    packet_copy.start()
     stream.next()
+    packet_copy.wait()
 
 
 def attend(args, dp_size):
-    query, keys, w_out, norm_gain = args[1], args[8], args[10], args[11]
+    query, keys, w_out, norm_gain, w_in = args[1], args[8], args[10], args[11], args[12]
     col_width = w_out.shape[1]
     tok_rows, head_local, head_dim = query.shape
     cache_len = keys.shape[2]
     width = head_local * head_dim + col_width + 2 * LANES
+    copies = 2 if tok_rows % 2 == 0 else tok_rows
     return pl.pallas_call(
         attend_kernel,
         out_shape=(
-            jax.ShapeDtypeStruct((dp_size, tok_rows, width), jnp.bfloat16),
+            pltpu.HBM((dp_size, tok_rows, width), jnp.bfloat16),
             pltpu.VMEM(w_out.shape, w_out.dtype),
             pltpu.VMEM(norm_gain.shape, norm_gain.dtype),
+            pltpu.VMEM((w_in.shape[2], in_cut_of(w_in)), w_in.dtype),
         ),
         in_specs=[pl.BlockSpec(memory_space=pl.ANY)] * len(args),
-        out_specs=(pl.BlockSpec(memory_space=pltpu.VMEM),) * 3,
-        scratch_shapes=[pltpu.VMEM(a.shape, a.dtype) for a in args[:10]]
+        out_specs=(pl.BlockSpec(memory_space=pl.ANY),)
+        + (pl.BlockSpec(memory_space=pltpu.VMEM),) * 3,
+        scratch_shapes=[pltpu.VMEM((dp_size, tok_rows, width), jnp.bfloat16)]
+        + [pltpu.VMEM(a.shape, a.dtype) for a in args[:10]]
         + [
             pltpu.VMEM((tok_rows, head_local, cache_len), jnp.float32),
-            pltpu.SemaphoreType.DMA((8,)),
-            pltpu.SemaphoreType.DMA((2 * tok_rows + 2,)),
+            pltpu.SemaphoreType.DMA((10,)),
+            pltpu.SemaphoreType.DMA((2 * copies + 2,)),
         ],
         compiler_params=pltpu.CompilerParams(vmem_limit_bytes=58 * MIB),
         cost_estimate=pl.CostEstimate(
@@ -222,11 +242,7 @@
     return places
 
 
-def project_kernel(came, w_out, norm_gain, w_in, packet, factors, early, rows, sems):
-    early_copy = pltpu.make_async_copy(
-        w_in.at[0, 0, :, pl.ds(0, early.shape[1])], early, sems.at[0]
-    )
-    early_copy.start()
+def project_kernel(came, w_out, norm_gain, packet, factors, rows):
     dp_size, tok_rows, width = came.shape
     depth, col_width = w_out.shape
     batch = dp_size * tok_rows
@@ -298,18 +314,13 @@
     factors[0] = jnp.broadcast_to(jnp.sum(weight, axis=1, keepdims=True), (slot_rows, LANES))
     first = (head_at == 0) & (dp_at % group_count == 0)
     factors[1] = jnp.full((slot_rows, LANES), jnp.where(first, 1.0 / TOP, 0.0))
-    early_copy.wait()
-
-
-def in_cut_of(w_in):
-    return 2 * LANES if w_in.shape[3] % (2 * LANES) == 0 else w_in.shape[3]
-
-
-def project(came, w_out, norm_gain, w_in, y_size):
+
+
+def project(came, w_out, norm_gain, y_size):
     dp_size, tok_rows = came.shape[:2]
     depth, col_width = w_out.shape
     slot_rows = dp_size * MOST
-    vmem, hbm = pl.BlockSpec(memory_space=pltpu.VMEM), pl.BlockSpec(memory_space=pl.ANY)
+    vmem = pl.BlockSpec(memory_space=pltpu.VMEM)
     return pl.pallas_call(
         project_kernel,
         out_shape=(
@@ -317,14 +328,10 @@
                 (dp_size * y_size, ROWS, slot_rows // ROWS * col_width + LANES), jnp.bfloat16
             ),
             jax.ShapeDtypeStruct((2, slot_rows, LANES), jnp.float32),
-            pltpu.VMEM((w_in.shape[2], in_cut_of(w_in)), w_in.dtype),
-        ),
-        in_specs=[vmem, vmem, vmem, hbm],
-        out_specs=(vmem, vmem, vmem),
-        scratch_shapes=[
-            pltpu.VMEM((dp_size * tok_rows, depth + col_width), jnp.float32),
-            pltpu.SemaphoreType.DMA((1,)),
-        ],
+        ),
+        in_specs=[vmem] * 3,
+        out_specs=(vmem, vmem),
+        scratch_shapes=[pltpu.VMEM((dp_size * tok_rows, depth + col_width), jnp.float32)],
         compiler_params=pltpu.CompilerParams(vmem_limit_bytes=58 * MIB),
         cost_estimate=pl.CostEstimate(
             flops=2 * dp_size * tok_rows * depth * col_width,
@@ -332,11 +339,7 @@
             transcendentals=0,
         ),
         name="project",
-    )(in_vmem(came), in_vmem(w_out), in_vmem(norm_gain), in_hbm(w_in))
-
-
-def cut_at(w_in, at, in_cut):
-    return w_in.at[0, at % 2, :, pl.ds(at // 2 * in_cut, in_cut)]
+    )(in_vmem(came), in_vmem(w_out), in_vmem(norm_gain))
 
 
 def early_kernel(arrived, w_in, early, sems):
@@ -433,7 +436,10 @@
             jnp.bfloat16
         )
     weight, part = factors[0, :, 0:1], factors[1, :, 0:1]
-    for j in range(down_count):
+    last = down_count - 1
+    if last == 0:
+        total[...] = jnp.zeros_like(total)
+    for j in range(last):
         stream.next()
         share = jnp.dot(
             hidden[:, j * down_cut : (j + 1) * down_cut],
@@ -443,7 +449,12 @@
         total[...] = share if j == 0 else total[...] + share
     for h in range(heads):
         cut = slice(h * feat_width, (h + 1) * feat_width)
-        given = weight * total[:, cut] + part * x[:, cut]
+        if h == 0:
+            stream.next()
+        share = jnp.dot(
+            hidden[:, last * down_cut :], downs[last, :, cut], preferred_element_type=jnp.float32
+        )
+        given = weight * (total[:, cut] + share) + part * x[:, cut]
         for o in range(slot_rows // most):
             out[o * heads + h] = given[o * most : (o + 1) * most].astype(jnp.bfloat16)
 
@@ -545,7 +556,7 @@
     dp_size, y_size = lax.axis_size("dp"), lax.axis_size("y")
     tok_rows, feat_width = residual.shape
 
-    sent, w_out, norm_gain = attend(
+    sent, w_out, norm_gain, first_in = attend(
         (
             lengths.reshape(1, tok_rows),
             query,
@@ -559,12 +570,13 @@
             value_cache,
             w_out,
             norm_gain.reshape(1, feat_width),
+            w_in,
         ),
         dp_size,
     )
     came = lax.all_to_all(sent, "dp", split_axis=0, concat_axis=0, tiled=True)
 
-    packet, factors, first_in = project(came, w_out, norm_gain, w_in, y_size)
+    packet, factors = project(came, w_out, norm_gain, y_size)
     arrived = lax.all_to_all(packet, ("dp", "y"), split_axis=0, concat_axis=0, tiled=True)
     swapped = lax.ppermute(arrived, "core", [(i, i ^ 1) for i in range(CORES)])
     early_in = load_early(arrived, w_in)

time: 64.6 us -> 62.9 us (0.974)
  Pallas kernels: 25.8 us -> 24.1 us
    pallas_call x1, Pallas kernels: 2.48 us -> 1.17 us  [project(): pl.pallas_call(project_kernel, out_shape=(jax.ShapeDtypeStruct((dp_size *...]
where the time goes in v3:
time: 62.9 us; the launch traced here: 62.5 us
  blocking collectives  38.4 us (61%)
  Pallas kernels  24.1 us (38%)
    all_to_all x1, blocking collectives, shards(): came = lax.all_to_all(sent, 'dp', split_axis=0, concat_axis=0, tiled=True)  14.5 us
    pallas_call x1, Pallas kernels, experts(): pl.pallas_call(expert_kernel, out_shape=jax.ShapeDtypeStruct((dp_size * (...  13.9 us
    all_to_all x1, blocking collectives, shards(): lax.all_to_all(packet, ('dp', 'y'), split_axis=0, concat_axis=0, tiled=True)  12.9 us
    all_to_all x1, blocking collectives, shards(): lax.all_to_all(given_back, ('dp', 'y', 'core'), split_axis=0, concat_axis...  10.9 us
    pallas_call x1, Pallas kernels, attend(): pl.pallas_call(attend_kernel, out_shape=(pltpu.HBM((dp_size, tok_rows, wi...  5.88 us
    pallas_call x1, Pallas kernels, load_early(): pl.pallas_call(early_kernel, out_shape=pltpu.VMEM(shape, w_in.dtype), in_...  2.27 us
  transfers between devices with their start and end apart: 1, of which 0 were waited for; matrix products, arithmetic and copies ran while one was open for 0% of the time, Pallas kernels for 4%

profile of v3, /device:TPU:0, one launch (start us, length us, event | category | flops | bytes accessed | tf_op | source)
XLA Modules:
  0.0 62.5 jit_solution(2874189525460314382)
XLA Ops:
  0.0 5.9 %attend.1 = (bf16[8,4,1792]{2,1,0:T(4,128)(2,1)}, bf16[1024,512]{1,0:T(8,128)(2,1)S(1)}, f32[1,1024]{1,0:T(1,128)S(1)}, bf16[4096,256]{1,0:T(8,128)(2,1)S(1)}) custom-call(s32[1,4]{1,0:T(1,128)} %bitcast.8, bf16[4,8,128]{2,1,0:T(8,128)(2,1)} %query_at.1, bf16[4,2,128]{2,1,0:T(2,128)(2,1)} %fresh_at.1, bf16[4,2,128]{2,1,0:T(2,128)(2,1)} %value_at.1, ...), custom_call_target="tpu_custom_call" | custom-call | flops 33554432 | bytes 9437184 | tf_op jit(solution)/shard_map/attend/pallas_call | solution.py:203
  5.9 14.5 %all_to_all.15.came = bf16[8,4,1792]{2,1,0:T(4,128)(2,1)S(1)} all-to-all(bf16[8,4,1792]{2,1,0:T(4,128)(2,1)} %get-tuple-element.11), channel_id=1, replica_groups=mesh['dp'=8,'y'=2,'core'=2] {'dp'}, dimensions={0} | all-to-all | bytes 229376 | tf_op jit(solution)/shard_map/all_to_all | solution.py:577
  20.4 1.2 %project.1 = (bf16[16,8,1152]{2,1,0:T(8,128)(2,1)}, f32[2,16,128]{2,1,0:T(8,128)}) custom-call(bf16[8,4,1792]{2,1,0:T(4,128)(2,1)S(1)} %all_to_all.15.came, bf16[1024,512]{1,0:T(8,128)(2,1)S(1)} %get-tuple-element.12.w_out, f32[1,1024]{1,0:T(1,128)S(1)} %get-tuple-element.13.norm_gain), custom_call_target="tpu_custom_call" | custom-call | flops 33554432 | bytes 1048576 | tf_op jit(solution)/shard_map/project/pallas_call | solution.py:324
  21.6 12.9 %all_to_all.16.arrived = bf16[16,8,1152]{2,1,0:T(8,128)(2,1)S(1)} all-to-all(bf16[16,8,1152]{2,1,0:T(8,128)(2,1)} %get-tuple-element.14), channel_id=1, replica_groups=mesh['dp'=8,'y'=2,'core'=2] {'dp','y'}, dimensions={0} | all-to-all | bytes 589824 | tf_op jit(solution)/shard_map/all_to_all | solution.py:580
  34.5 0.0 copy-start
  34.5 0.0 collective-permute-start
  34.5 2.3 %load_early.1.early_in = bf16[2,4096,256]{2,1,0:T(8,128)(2,1)S(1)} custom-call(bf16[16,8,1152]{2,1,0:T(8,128)(2,1)S(1)} %all_to_all.16.arrived, bf16[1,2,4096,1792]{3,2,1,0:T(8,128)(2,1)} %w_in.5), custom_call_target="tpu_custom_call" | custom-call | flops 67108864 | bytes 4194304 | tf_op jit(solution)/shard_map/load_early/pallas_call | solution.py:360
  36.8 0.0 collective-permute-done.swapped
  36.8 0.0 copy-done
  36.8 0.0 copy-start.1
  36.8 13.9 %experts.1 = bf16[32,2,1024]{2,1,0:T(2,128)(2,1)} custom-call(bf16[16,8,1152]{2,1,0:T(8,128)(2,1)S(1)} %all_to_all.16.arrived, bf16[16,8,1152]{2,1,0:T(8,128)(2,1)S(1)} %collective-permute-done.swapped, f32[2,16,128]{2,1,0:T(8,128)S(1)} %copy-done, bf16[4096,256]{1,0:T(8,128)(2,1)S(1)} %get-tuple-element.16.first_in, ...), custom_call_target="tpu_custom_call" | custom-call | flops 704643072 | bytes 44040192 | tf_op jit(solution)/shard_map/experts/pallas_call | solution.py:468
  50.7 10.9 %all_to_all.17.back = bf16[32,2,1024]{2,1,0:T(2,128)(2,1)S(1)} all-to-all(bf16[32,2,1024]{2,1,0:T(2,128)(2,1)} %experts.1), channel_id=1, replica_groups=mesh['dp'=8,'y'=2,'core'=2] {'dp','y','core'}, dimensions={0} | all-to-all | bytes 262144 | tf_op jit(solution)/shard_map/all_to_all | solution.py:587
  61.6 0.0 copy-done.1
  61.6 0.9 %combine.1 = bf16[4,1024]{1,0:T(4,128)(2,1)} custom-call(bf16[32,2,1024]{2,1,0:T(2,128)(2,1)S(1)} %all_to_all.17.back, s32[2,4]{1,0:T(2,128)S(1)} %bitcast.5), custom_call_target="tpu_custom_call" | custom-call | flops 524288 | bytes 131072 | tf_op jit(solution)/shard_map/combine/pallas_call | solution.py:526
Async XLA Ops:
  34.5 2.3 %copy-start = (f32[2,16,128]{2,1,0:T(8,128)S(1)}, f32[2,16,128]{2,1,0:T(8,128)}, u32[]{:S(2)}) copy-start(f32[2,16,128]{2,1,0:T(8,128)} %get-tuple-element.15.factors) | copy-start | bytes 49156
  34.5 2.3 %collective-permute-start = (bf16[16,8,1152]{2,1,0:T(8,128)(2,1)S(1)}, bf16[16,8,1152]{2,1,0:T(8,128)(2,1)S(1)}, u32[]{:S(2)}, u32[]{:S(2)}) collective-permute-start(bf16[16,8,1152]{2,1,0:T(8,128)(2,1)S(1)} %all_to_all.16.arrived), channel_id=1, source_target_pairs={{0,1},{1,0},{2,3},{3,2},{4,5},{5,4},{6,7},{7,6},{8,9},{9,8},{10,11... | collective-permute-start | bytes 884744 | tf_op jit(solution)/shard_map/ppermute | solution.py:581
  36.8 24.8 %copy-start.1 = (s32[4,2]{0,1:T(2,128)S(1)}, s32[4,2]{0,1:T(2,128)}, u32[]{:S(2)}) copy-start(s32[4,2]{0,1:T(2,128)} %param.24) | copy-start | bytes 100

commit v4 on v3

--- a/solution.py
+++ b/solution.py
@@ -17,7 +17,7 @@
 EPSILON = 1e-05
 MIB = 2**20
 AHEAD = 4
-EARLY = 3
+EARLY = 2
 
 
 def in_hbm(x):

time: 62.9 us -> 62.2 us (0.989)
    pallas_call x1, Pallas kernels: 2.27 us -> 1.61 us  [load_early(): pl.pallas_call(early_kernel, out_shape=pltpu.VMEM(shape, w_in.dtype), in_...]
  transfers between devices with their start and end apart: 1 -> 1, of which waited for: 0 -> 0; matrix products, arithmetic and copies ran while one was open for 0% -> 0% of each run, Pallas kernels for 4% -> 3%
where the time goes in v4:
time: 62.2 us; the launch traced here: 61.9 us
  blocking collectives  38.1 us (61%)
  Pallas kernels  23.7 us (38%)
    all_to_all x1, blocking collectives, shards(): came = lax.all_to_all(sent, 'dp', split_axis=0, concat_axis=0, tiled=True)  14.5 us
    pallas_call x1, Pallas kernels, experts(): pl.pallas_call(expert_kernel, out_shape=jax.ShapeDtypeStruct((dp_size * (...  14.1 us
    all_to_all x1, blocking collectives, shards(): lax.all_to_all(packet, ('dp', 'y'), split_axis=0, concat_axis=0, tiled=True)  12.9 us
    all_to_all x1, blocking collectives, shards(): lax.all_to_all(given_back, ('dp', 'y', 'core'), split_axis=0, concat_axis...  10.7 us
    pallas_call x1, Pallas kernels, attend(): pl.pallas_call(attend_kernel, out_shape=(pltpu.HBM((dp_size, tok_rows, wi...  5.88 us
    pallas_call x1, Pallas kernels, load_early(): pl.pallas_call(early_kernel, out_shape=pltpu.VMEM(shape, w_in.dtype), in_...  1.61 us
  transfers between devices with their start and end apart: 1, of which 0 were waited for; matrix products, arithmetic and copies ran while one was open for 0% of the time, Pallas kernels for 3%

profile of v4, /device:TPU:0, one launch (start us, length us, event | category | flops | bytes accessed | tf_op | source)
XLA Modules:
  0.0 61.9 jit_solution(9472560163818869991)
XLA Ops:
  0.0 5.9 %attend.1 = (bf16[8,4,1792]{2,1,0:T(4,128)(2,1)}, bf16[1024,512]{1,0:T(8,128)(2,1)S(1)}, f32[1,1024]{1,0:T(1,128)S(1)}, bf16[4096,256]{1,0:T(8,128)(2,1)S(1)}) custom-call(s32[1,4]{1,0:T(1,128)} %bitcast.8, bf16[4,8,128]{2,1,0:T(8,128)(2,1)} %query_at.1, bf16[4,2,128]{2,1,0:T(2,128)(2,1)} %fresh_at.1, bf16[4,2,128]{2,1,0:T(2,128)(2,1)} %value_at.1, ...), custom_call_target="tpu_custom_call" | custom-call | flops 33554432 | bytes 9437184 | tf_op jit(solution)/shard_map/attend/pallas_call | solution.py:203
  5.9 14.5 %all_to_all.15.came = bf16[8,4,1792]{2,1,0:T(4,128)(2,1)S(1)} all-to-all(bf16[8,4,1792]{2,1,0:T(4,128)(2,1)} %get-tuple-element.11), channel_id=1, replica_groups=mesh['dp'=8,'y'=2,'core'=2] {'dp'}, dimensions={0} | all-to-all | bytes 229376 | tf_op jit(solution)/shard_map/all_to_all | solution.py:577
  20.4 1.2 %project.1 = (bf16[16,8,1152]{2,1,0:T(8,128)(2,1)}, f32[2,16,128]{2,1,0:T(8,128)}) custom-call(bf16[8,4,1792]{2,1,0:T(4,128)(2,1)S(1)} %all_to_all.15.came, bf16[1024,512]{1,0:T(8,128)(2,1)S(1)} %get-tuple-element.12.w_out, f32[1,1024]{1,0:T(1,128)S(1)} %get-tuple-element.13.norm_gain), custom_call_target="tpu_custom_call" | custom-call | flops 33554432 | bytes 1048576 | tf_op jit(solution)/shard_map/project/pallas_call | solution.py:324
  21.6 12.9 %all_to_all.16.arrived = bf16[16,8,1152]{2,1,0:T(8,128)(2,1)S(1)} all-to-all(bf16[16,8,1152]{2,1,0:T(8,128)(2,1)} %get-tuple-element.14), channel_id=1, replica_groups=mesh['dp'=8,'y'=2,'core'=2] {'dp','y'}, dimensions={0} | all-to-all | bytes 589824 | tf_op jit(solution)/shard_map/all_to_all | solution.py:580
  34.5 0.0 copy-start
  34.5 0.0 collective-permute-start
  34.5 1.6 %load_early.1.early_in = bf16[1,4096,256]{2,1,0:T(8,128)(2,1)S(1)} custom-call(bf16[16,8,1152]{2,1,0:T(8,128)(2,1)S(1)} %all_to_all.16.arrived, bf16[1,2,4096,1792]{3,2,1,0:T(8,128)(2,1)} %w_in.5), custom_call_target="tpu_custom_call" | custom-call | flops 33554432 | bytes 2097152 | tf_op jit(solution)/shard_map/load_early/pallas_call | solution.py:360
  36.1 0.0 collective-permute-done.swapped
  36.1 0.0 copy-done
  36.1 0.0 copy-start.1
  36.2 14.1 %experts.1 = bf16[32,2,1024]{2,1,0:T(2,128)(2,1)S(1)} custom-call(bf16[16,8,1152]{2,1,0:T(8,128)(2,1)S(1)} %all_to_all.16.arrived, bf16[16,8,1152]{2,1,0:T(8,128)(2,1)S(1)} %collective-permute-done.swapped, f32[2,16,128]{2,1,0:T(8,128)S(1)} %copy-done, bf16[4096,256]{1,0:T(8,128)(2,1)S(1)} %get-tuple-element.16.first_in, ...), custom_call_target="tpu_custom_call" | custom-call | flops 704643072 | bytes 44040192 | tf_op jit(solution)/shard_map/experts/pallas_call | solution.py:468
  50.3 10.7 %all_to_all.17.back = bf16[32,2,1024]{2,1,0:T(2,128)(2,1)S(1)} all-to-all(bf16[32,2,1024]{2,1,0:T(2,128)(2,1)S(1)} %experts.1), channel_id=1, replica_groups=mesh['dp'=8,'y'=2,'core'=2] {'dp','y','core'}, dimensions={0} | all-to-all | bytes 262144 | tf_op jit(solution)/shard_map/all_to_all | solution.py:587
  61.0 0.0 copy-done.1
  61.0 0.9 %combine.1 = bf16[4,1024]{1,0:T(4,128)(2,1)} custom-call(bf16[32,2,1024]{2,1,0:T(2,128)(2,1)S(1)} %all_to_all.17.back, s32[2,4]{1,0:T(2,128)S(1)} %bitcast.5), custom_call_target="tpu_custom_call" | custom-call | flops 524288 | bytes 131072 | tf_op jit(solution)/shard_map/combine/pallas_call | solution.py:526
Async XLA Ops:
  34.5 1.6 %copy-start = (f32[2,16,128]{2,1,0:T(8,128)S(1)}, f32[2,16,128]{2,1,0:T(8,128)}, u32[]{:S(2)}) copy-start(f32[2,16,128]{2,1,0:T(8,128)} %get-tuple-element.15.factors) | copy-start | bytes 49156
  34.5 1.6 %collective-permute-start = (bf16[16,8,1152]{2,1,0:T(8,128)(2,1)S(1)}, bf16[16,8,1152]{2,1,0:T(8,128)(2,1)S(1)}, u32[]{:S(2)}, u32[]{:S(2)}) collective-permute-start(bf16[16,8,1152]{2,1,0:T(8,128)(2,1)S(1)} %all_to_all.16.arrived), channel_id=1, source_target_pairs={{0,1},{1,0},{2,3},{3,2},{4,5},{5,4},{6,7},{7,6},{8,9},{9,8},{10,11... | collective-permute-start | bytes 884744 | tf_op jit(solution)/shard_map/ppermute | solution.py:581
  36.1 24.8 %copy-start.1 = (s32[4,2]{0,1:T(2,128)S(1)}, s32[4,2]{0,1:T(2,128)}, u32[]{:S(2)}) copy-start(s32[4,2]{0,1:T(2,128)} %param.24) | copy-start | bytes 100
